TPU v7x, 32 devices: a whole 2x2x4 slice. The times are simulated.
32 devices in a mesh: tp: 4 (over z), dp: 2 (over y), pp: 4 (over x, core).
Axes of the slice: x: 2, y: 2, z: 4, core: 2. Of those that a mesh axis runs over, the one named last changes fastest.
Arguments:
- master: float32 [50304, 768], P('tp')
- exp_avg: float32 [50304, 768], P('tp')
- exp_avg_sq: float32 [50304, 768], P('tp')
- stage_ids: int32 [4, 16, 384], P('pp', 'dp')
- stage_acts: bfloat16 [4, 16, 384, 768], P('pp', 'dp')
Outputs:
- output 1: float32 [50304, 768], P('tp')
- output 2: float32 [50304, 768], P('tp')
- output 3: float32 [50304, 768], P('tp')
- output 4: bfloat16 [50304, 768], P('tp')
All inputs are finite; a program needn't handle non-finite values.
Results may differ from a plain program's by a relative error of at most 0.001.
Values sent between devices are 32-bit elements.
A program may use at most 1 GiB of HBM per device.

v0:
```python
import functools

import jax
import jax.numpy as jnp
from jax import lax
from jax.experimental import pallas as pl
from jax.experimental.pallas import tpu as pltpu
from jax.sharding import PartitionSpec as P


LEARN_RATE = 0.003
BETA_ONE = 0.9
BETA_TWO = 0.95
ADAM_EPS = 1e-8
WEIGHT_DECAY = 0.1
CLIP_NORM = 1.0
OPT_STEP = 10

ROW_STEP = 264
TOK_STEP = 512
ADAMW_DEPTH = 4
ADAMW_FLOPS = 2000
VMEM_LIMIT = 60 * 1024 * 1024


def dot_nt(a, b):
    return lax.dot_general(a, b, (((1,), (1,)), ((), ())), preferred_element_type=jnp.float32)


SPREAD_CHUNKS = 24
MESH = pl.DeviceIdType.MESH


def spread_kernel(act_ref, ids_ref, hid_ref, look_ref, all_ids_ref, buf, ids_buf, sx, sy, sz, sd, sl, si, load, recv, recv_core, recv_ids):
    z, y, p = lax.axis_index("tp"), lax.axis_index("dp"), lax.axis_index("pp")
    x, core, odd = p // 2, p % 2, z % 2
    x_dev = {"pp": (1 - x) * 2 + core}
    y_dev = {"dp": 1 - y}
    z_dev = {"tp": z + 1 - 2 * odd}
    core_dev = {"pp": x * 2 + 1 - core}
    plane = [{"dp": (y + dy) % 2, "pp": (p + dp) % 4} for dy in range(2) for dp in range(4) if dy + dp > 0]
    n = SPREAD_CHUNKS
    edge, main = n // 3, 2 * n // 3
    tok = act_ref.shape[0]
    size = tok // n

    barrier = pltpu.get_barrier_semaphore()
    for dev in plane + [z_dev]:
        pl.semaphore_signal(barrier, inc=1, device_id=dev, device_id_type=MESH)
    pl.semaphore_wait(barrier, len(plane) + 1)

    def chunk(i):
        if i < edge:
            return odd * main + i
        return i if i < main else (1 - odd) * main + (i - main)

    def span(replica, i):
        return pl.ds(pl.multiple_of(replica * tok + chunk(i) * size, size), size)

    def remote(src, dst, send_sem, recv_sem, dev):
        copy = pltpu.make_async_remote_copy(src_ref=src, dst_ref=dst, send_sem=send_sem, recv_sem=recv_sem, device_id=dev, device_id_type=MESH)
        copy.start()
        return copy

    def send_ids(kind):
        local = pltpu.make_async_copy(ids_ref, ids_buf.at[kind, y], recv_ids.at[kind, y])
        local.start()
        for i, dev in enumerate(plane):
            remote(ids_ref, ids_buf.at[kind, y], si.at[i], recv_ids.at[kind, y], dev)

    def drain_ids():
        for i in range(len(plane)):
            pltpu.make_async_copy(ids_ref, ids_ref, si.at[i]).wait()

    pl.when(p == 0)(lambda: send_ids(0))
    pl.when(p == 3)(lambda: send_ids(1))

    def run(out_ref, x_src):

        def send(replica, i, send_sem, recv_sem, dev):
            view = buf.at[span(replica, i)]
            return remote(view, view, send_sem, recv_sem, dev)

        def arrived(replica, i, slot):
            view = buf.at[span(replica, i)]
            pltpu.make_async_copy(view, view, recv.at[slot, i]).wait()

        def keep(copies, replica, i, slot):
            view, place = buf.at[span(replica, i)], out_ref.at[span(replica, i)]
            copies.append(remote(view, place, sd.at[slot, i], recv_core.at[slot, i], core_dev).wait_send)
            local = pltpu.make_async_copy(view, place, sl.at[slot, i])
            local.start()
            copies.append(local.wait)

        @pl.when(x == x_src)
        def _():
            copies, loads = [], []
            for i in range(n):
                rows = pl.ds(pl.multiple_of(chunk(i) * size, size), size)
                loads.append(pltpu.make_async_copy(act_ref.at[rows], buf.at[span(y, i)], load.at[i]))
                loads[-1].start()
            for i in range(n):
                loads[i].wait()
                if i < edge:
                    copies.append(send(y, i, sx.at[i], recv.at[0, i], x_dev).wait_send)
                if i < main:
                    copies.append(send(y, i, sy.at[i], recv.at[1, i], y_dev).wait_send)
            for i in range(n):
                keep(copies, y, i, 0)
            for i in range(main):
                arrived(1 - y, i, 1)
                if i + edge < main:
                    copies.append(send(y, i + edge, sx.at[i + edge], recv.at[0, i + edge], x_dev).wait_send)
                if i % 2 == 0:
                    copies.append(send(1 - y, i, sx.at[main + i // 2], recv.at[1, i], x_dev).wait_send)
                if i < edge:
                    copies.append(send(1 - y, i, sz.at[1, i], recv.at[1, main + i], z_dev).wait_send)
                keep(copies, 1 - y, i, 1)
            for i in range(main, n):
                arrived(1 - y, i, 1)
                keep(copies, 1 - y, i, 1)
            for wait in copies:
                wait()

        @pl.when(x != x_src)
        def _():
            copies = []
            for s in range(main + edge):
                if s < main:
                    arrived(y, s, 0)
                    if s % 2 == 1:
                        copies.append(send(y, s, sy.at[s], recv.at[1, s], y_dev).wait_send)
                    if s < edge:
                        copies.append(send(y, s, sz.at[0, s], recv.at[0, main + s], z_dev).wait_send)
                    keep(copies, y, s, 0)
                if s >= edge:
                    i = s - edge
                    arrived(1 - y, i, 1)
                    if i < edge:
                        copies.append(send(1 - y, i, sz.at[1, i], recv.at[1, main + i], z_dev).wait_send)
                    keep(copies, 1 - y, i, 1)
            for i in range(main, n):
                for slot, replica in ((0, y), (1, 1 - y)):
                    arrived(replica, i, slot)
                    keep(copies, replica, i, slot)
            for wait in copies:
                wait()

    def wait_core(out_ref):
        for slot, replica in ((0, y), (1, 1 - y)):
            for i in range(n):
                view = out_ref.at[span(replica, i)]
                pltpu.make_async_copy(view, view, recv_core.at[slot, i]).wait()

    @pl.when(core == 1)
    def _():
        run(hid_ref, 1)
        wait_core(look_ref)

    @pl.when(core == 0)
    def _():
        run(look_ref, 0)
        wait_core(hid_ref)

    for kind in range(2):
        for replica in range(2):
            pltpu.make_async_copy(ids_ref, ids_buf.at[kind, replica], recv_ids.at[kind, replica]).wait()
    pl.when(p == 0)(drain_ids)
    pl.when(p == 3)(drain_ids)
    all_ids_ref[...] = ids_buf[...]


def spread_call(acts, ids, n_repl):
    tok, dim = acts.shape
    n = SPREAD_CHUNKS
    shape = jax.ShapeDtypeStruct((n_repl * tok, dim), jnp.float32)
    ids_shape = (2, n_repl) + ids.shape
    dma = pltpu.SemaphoreType.DMA
    return pl.pallas_call(
        spread_kernel,
        in_specs=[pl.BlockSpec(memory_space=pl.ANY), pl.BlockSpec(memory_space=pltpu.VMEM)],
        out_specs=[pl.BlockSpec(memory_space=pl.ANY)] * 2 + [pl.BlockSpec(memory_space=pltpu.VMEM)],
        out_shape=[shape, shape, jax.ShapeDtypeStruct(ids_shape, jnp.int32)],
        scratch_shapes=[
            pltpu.VMEM((n_repl * tok, dim), jnp.float32), pltpu.VMEM(ids_shape, jnp.int32),
            dma((n + n // 2,)), dma((n,)), dma((2, n // 3)), dma((2, n)), dma((2, n)), dma((8,)),
            dma((n,)), dma((2, n)), dma((2, n)), dma((2, 2)),
        ],
        compiler_params=pltpu.CompilerParams(collective_id=0, has_side_effects=True, vmem_limit_bytes=VMEM_LIMIT),
        name="spread",
    )(acts, ids)


def slice_partners(z, y, p):
    return [
        {"pp": (p // 2) * 2 + 1 - p % 2}, {"pp": (1 - p // 2) * 2 + p % 2}, {"dp": 1 - y},
        {"tp": z + 1 - 2 * (z % 2)}, {"tp": (z + 2) % 4},
    ]


def meet(partners):
    barrier = pltpu.get_barrier_semaphore()
    for dev in partners:
        pl.semaphore_signal(barrier, inc=1, device_id=dev, device_id_type=MESH)
    pl.semaphore_wait(barrier, len(partners))


def combine_kernel(scale, in_ref, top_ref, inv_ref, mine, theirs, send_sem, recv_sem):
    z, y, p = lax.axis_index("tp"), lax.axis_index("dp"), lax.axis_index("pp")
    partners = slice_partners(z, y, p)
    meet(partners)
    half = in_ref.shape[0] // 2
    mine[0] = in_ref[...]
    for step, dev in enumerate(partners):
        copy = pltpu.make_async_remote_copy(src_ref=mine.at[step], dst_ref=theirs.at[step], send_sem=send_sem.at[step], recv_sem=recv_sem.at[step], device_id=dev, device_id_type=MESH)
        copy.start()
        copy.wait()
        top_a, sum_a = mine[step, :half], mine[step, half:]
        top_b, sum_b = theirs[step, :half], theirs[step, half:]
        top = jnp.maximum(top_a, top_b)
        total = sum_a * jnp.exp(top_a - top) + sum_b * jnp.exp(top_b - top)
        if step + 1 < len(partners):
            mine[step + 1, :half] = top
            mine[step + 1, half:] = total
        else:
            top_ref[...] = top
            inv_ref[...] = 1.0 / (total * scale)


def combine_call(local, scale):
    rows, lanes = local.shape
    shape = jax.ShapeDtypeStruct((rows // 2, lanes), jnp.float32)
    return pl.pallas_call(
        functools.partial(combine_kernel, scale),
        in_specs=[pl.BlockSpec(memory_space=pltpu.VMEM)],
        out_specs=[pl.BlockSpec(memory_space=pltpu.VMEM)] * 2,
        out_shape=[shape, shape],
        scratch_shapes=[pltpu.VMEM((5, rows, lanes), jnp.float32), pltpu.VMEM((5, rows, lanes), jnp.float32), pltpu.SemaphoreType.DMA((5,)), pltpu.SemaphoreType.DMA((5,))],
        compiler_params=pltpu.CompilerParams(collective_id=1, has_side_effects=True),
        name="combine",
    )(local)


def stats_kernel(scal_ref, master_ref, act_ref, max_ref, sum_ref, cast_ref, *table_refs):
    @pl.when(pl.program_id(0) == 0)
    def _():
        start = 0
        for ref in table_refs:
            ref[...] = master_ref[start:start + ref.shape[0], :].astype(jnp.bfloat16)
            start += ref.shape[0]

    act = act_ref[...].astype(jnp.bfloat16)
    cast_ref[...] = act
    rows = master_ref.shape[0]
    tiles = [ref[i:i + ROW_STEP, :] for ref in table_refs for i in range(0, ref.shape[0], ROW_STEP)]
    parts = []
    for start, tile in zip(range(0, rows, ROW_STEP), tiles):
        logits = dot_nt(tile, act)
        if start + ROW_STEP == rows:
            row = start + lax.broadcasted_iota(jnp.int32, logits.shape, 0)
            logits = jnp.where(row < scal_ref[1], logits, -jnp.inf)
        top = jnp.max(logits, axis=0, keepdims=True)
        parts.append((top, jnp.sum(jnp.exp(logits - top), axis=0, keepdims=True)))
    top_all = functools.reduce(jnp.maximum, [p[0] for p in parts])
    max_ref[...] = top_all
    sum_ref[...] = functools.reduce(jnp.add, [p[1] * jnp.exp(p[0] - top_all) for p in parts])


def stats_call(scal, master, splits, acts):
    tokens, dim = acts.shape
    rows = sum(splits)
    return pl.pallas_call(
        stats_kernel,
        grid_spec=pltpu.PrefetchScalarGridSpec(
            num_scalar_prefetch=1,
            grid=(tokens // TOK_STEP,),
            in_specs=[
                pl.BlockSpec((rows, dim), lambda t, scal: (scal[2], 0), pipeline_mode=pl.Buffered(1)),
                pl.BlockSpec((TOK_STEP, dim), lambda t, scal: (t, 0)),
            ],
            out_specs=[
                pl.BlockSpec((1, TOK_STEP), lambda t, scal: (0, t)),
                pl.BlockSpec((1, TOK_STEP), lambda t, scal: (0, t)),
                pl.BlockSpec((TOK_STEP, dim), lambda t, scal: (t, 0)),
            ] + [pl.BlockSpec((part, dim), lambda t, scal: (0, 0)) for part in splits],
        ),
        out_shape=[
            jax.ShapeDtypeStruct((1, tokens), jnp.float32),
            jax.ShapeDtypeStruct((1, tokens), jnp.float32),
            jax.ShapeDtypeStruct((tokens, dim), jnp.bfloat16),
        ] + [jax.ShapeDtypeStruct((part, dim), jnp.bfloat16) for part in splits],
        compiler_params=pltpu.CompilerParams(vmem_limit_bytes=VMEM_LIMIT),
        cost_estimate=pl.CostEstimate(flops=2 * tokens * rows * dim, bytes_accessed=6 * tokens * dim, transcendentals=tokens * rows),
        name="stats",
    )(scal, master, acts)


def norm_kernel(n_dev, *refs):
    *in_refs, out_ref, mine, theirs, send_sem, recv_sem = refs
    z, y, p = lax.axis_index("tp"), lax.axis_index("dp"), lax.axis_index("pp")
    n_tp, n_repl, n_stage = n_dev
    steps = [(a, b, c) for a in range(n_tp) for b in range(n_repl) for c in range(n_stage)][1:]
    devices = [{"tp": (z + a) % n_tp, "dp": (y + b) % n_repl, "pp": (p + c) % n_stage} for a, b, c in steps]
    meet(devices)
    mine[...] = jnp.full(mine.shape, jnp.sum(sum(ref[...] for ref in in_refs)))
    me = (z * n_repl + y) * n_stage + p
    copies = []
    for i, dev in enumerate(devices):
        copy = pltpu.make_async_remote_copy(src_ref=mine, dst_ref=theirs.at[me], send_sem=send_sem.at[i], recv_sem=recv_sem.at[me], device_id=dev, device_id_type=MESH)
        copy.start()
        copies.append(copy)
    own = pltpu.make_async_copy(mine, theirs.at[me], recv_sem.at[me])
    own.start()
    for i in range(len(steps) + 1):
        pltpu.make_async_copy(mine, theirs.at[i], recv_sem.at[i]).wait()
    for copy in copies:
        copy.wait_send()
    total = jnp.sum(theirs[...], axis=0)
    out_ref[...] = CLIP_NORM / jnp.maximum(jnp.sqrt(total), CLIP_NORM)


def norm_call(squares, n_dev):
    n_all = n_dev[0] * n_dev[1] * n_dev[2]
    vmem = pl.BlockSpec(memory_space=pltpu.VMEM)
    return pl.pallas_call(
        functools.partial(norm_kernel, n_dev),
        in_specs=[vmem] * len(squares),
        out_specs=vmem,
        out_shape=jax.ShapeDtypeStruct((8, 128), jnp.float32),
        scratch_shapes=[pltpu.VMEM((8, 128), jnp.float32), pltpu.VMEM((n_all, 8, 128), jnp.float32), pltpu.SemaphoreType.DMA((n_all,)), pltpu.SemaphoreType.DMA((n_all,))],
        compiler_params=pltpu.CompilerParams(collective_id=2, has_side_effects=True),
        name="norm",
    )(*squares)


def grad_kernel(offset, tok_count, scal_ref, table_ref, hid_ref, dx_ref, max_ref, inv_ref, lab_ref, ids_ref, *out_refs):
    *grad_refs, sq_ref = out_refs
    step = pl.program_id(0)
    rows = grad_refs[0].shape[0]

    @pl.when(step == 0)
    def _():
        for grad_ref in grad_refs:
            grad_ref[...] = jnp.zeros_like(grad_ref)

    hid = hid_ref[...]
    look = dx_ref[...].astype(jnp.bfloat16)
    for start in range(0, rows * len(grad_refs), ROW_STEP):
        logits = dot_nt(table_ref[start:start + ROW_STEP, :], hid)
        local = offset + start + lax.broadcasted_iota(jnp.int32, logits.shape, 0)
        row = jnp.where(local < scal_ref[1], local + scal_ref[0], -1)
        prob = jnp.where(local < scal_ref[1], jnp.exp(logits - max_ref[...]) * inv_ref[...], 0.0)
        dlog = (prob - jnp.where(row == lab_ref[...], 1.0 / tok_count, 0.0)).astype(jnp.bfloat16)
        hot = jnp.where(row == ids_ref[...], 1.0, 0.0).astype(jnp.bfloat16)
        part = jnp.dot(dlog, hid, preferred_element_type=jnp.float32)
        part += jnp.dot(hot, look, preferred_element_type=jnp.float32)
        grad_refs[start // rows][start % rows:start % rows + ROW_STEP, :] += part

    @pl.when(step == pl.num_programs(0) - 1)
    def _():
        square = jnp.zeros_like(sq_ref)
        for grad_ref in grad_refs:
            grad = grad_ref[...] * 0.5
            grad_ref[...] = grad
            square += jnp.sum(grad * grad, axis=0, keepdims=True)
        sq_ref[...] = square


def grad_call(scal, table_bf, hid, dx, top, inv, labels, ids, offset, tok_count):
    tokens, dim = hid.shape
    rows, n_out = table_bf.shape[0], 1
    tok_spec = pl.BlockSpec((1, TOK_STEP), lambda t: (0, t))
    act_spec = pl.BlockSpec((TOK_STEP, dim), lambda t: (t, 0))
    return pl.pallas_call(
        functools.partial(grad_kernel, offset, tok_count),
        grid=(tokens // TOK_STEP,),
        in_specs=[
            pl.BlockSpec(memory_space=pltpu.SMEM),
            pl.BlockSpec((rows * n_out, dim), lambda t: (0, 0)),
            act_spec, act_spec, tok_spec, tok_spec, tok_spec, tok_spec,
        ],
        out_specs=[pl.BlockSpec((rows, dim), lambda t: (0, 0))] * n_out + [pl.BlockSpec((1, dim), lambda t: (0, 0))],
        out_shape=[jax.ShapeDtypeStruct((rows, dim), jnp.float32)] * n_out + [jax.ShapeDtypeStruct((1, dim), jnp.float32)],
        compiler_params=pltpu.CompilerParams(vmem_limit_bytes=VMEM_LIMIT),
        cost_estimate=pl.CostEstimate(flops=6 * tokens * rows * n_out * dim, bytes_accessed=6 * tokens * dim, transcendentals=tokens * rows * n_out),
    )(scal, table_bf, hid, dx, top, inv, labels, ids)


def adamw_kernel(counts, spots, n_alias, *refs):
    n_piece = len(counts)
    scale_ref = refs[0]
    state_refs = refs[1:4]
    piece_refs = refs[4:4 + n_piece]
    *out_refs, out_scale, in_buf, out_buf, bf_buf, in_sem, out_sem = refs[4 + n_piece + n_alias:]
    y, p = lax.axis_index("dp"), lax.axis_index("pp")
    x, core = p // 2, p % 2
    out_scale[...] = scale_ref[...]
    scale = scale_ref[0:1, 0:1]
    vocab = state_refs[0].shape[0]
    depth, short, sub_rows = in_buf.shape[0], vocab % ROW_STEP, 24
    blocks = [(j, i) for j, count in enumerate(counts) for i in range(count)]

    def by_length(row, action):
        if short == 0:
            action(ROW_STEP)
        else:
            pl.when(row + ROW_STEP <= vocab)(lambda: action(ROW_STEP))
            pl.when(row + ROW_STEP > vocab)(lambda: action(short))

    def first_row(b):
        j, i = blocks[b]
        flip_y, flip_x, flip_core, block = spots[j]
        yy, xx, cc = (1 - v if flip else v for v, flip in ((y, flip_y), (x, flip_x), (core, flip_core)))
        own_blocks = -(-vocab // (8 * ROW_STEP))
        return pl.multiple_of(((yy * 4 + xx * 2 + cc) * own_blocks + block + i) * ROW_STEP, 8)

    def grad_copy(b):
        j, i = blocks[b]
        return pltpu.make_async_copy(piece_refs[j].at[pl.ds(i * ROW_STEP, ROW_STEP)], in_buf.at[b % depth, 3], in_sem.at[b % depth, 3])

    def in_copies(b, row, size):
        slot = b % depth
        return [pltpu.make_async_copy(ref.at[pl.ds(row, size)], in_buf.at[slot, k, pl.ds(0, size)], in_sem.at[slot, k]) for k, ref in enumerate(state_refs)]

    def out_copies(b, row, size):
        slot = b % depth
        sources = [out_buf.at[slot, k] for k in range(3)] + [bf_buf.at[slot]]
        return [pltpu.make_async_copy(src.at[pl.ds(0, size)], ref.at[pl.ds(row, size)], out_sem.at[slot, k]) for k, (src, ref) in enumerate(zip(sources, out_refs))]

    def each(make, b, method):
        row = first_row(b)

        def act(size):
            for copy in make(b, row, size):
                getattr(copy, method)()

        by_length(row, act)

    def start_in(b):
        each(in_copies, b, "start")
        grad_copy(b).start()

    for b in range(min(depth - 1, len(blocks))):
        start_in(b)
    for b in range(len(blocks)):
        if b + depth - 1 < len(blocks):
            start_in(b + depth - 1)
        each(in_copies, b, "wait")
        grad_copy(b).wait()
        if b >= depth:
            each(out_copies, b - depth, "wait")
        slot = b % depth

        def body(i, carry):
            rows = pl.ds(pl.multiple_of(i * sub_rows, 8), sub_rows)
            grad = in_buf[slot, 3, rows, :] * scale
            avg = BETA_ONE * in_buf[slot, 1, rows, :] + (1.0 - BETA_ONE) * grad
            sq = BETA_TWO * in_buf[slot, 2, rows, :] + (1.0 - BETA_TWO) * grad * grad
            step_dir = (avg / (1.0 - BETA_ONE ** OPT_STEP)) / (jnp.sqrt(sq / (1.0 - BETA_TWO ** OPT_STEP)) + ADAM_EPS)
            old = in_buf[slot, 0, rows, :]
            new = old - LEARN_RATE * (step_dir + WEIGHT_DECAY * old)
            out_buf[slot, 0, rows, :] = new
            out_buf[slot, 1, rows, :] = avg
            out_buf[slot, 2, rows, :] = sq
            bf_buf[slot, rows, :] = new.astype(jnp.bfloat16)
            return carry

        lax.fori_loop(0, ROW_STEP // sub_rows, body, 0)
        each(out_copies, b, "start")
    for b in range(max(0, len(blocks) - depth), len(blocks)):
        each(out_copies, b, "wait")


def adamw_call(scale, state, pieces, spots, outs):
    vocab, dim = state[0].shape
    counts = tuple(p.shape[0] // ROW_STEP for p in pieces)
    extra = list(outs) if outs is not None else []
    n_in = 1 + 3 + len(pieces)
    shapes = [jax.ShapeDtypeStruct((vocab, dim), jnp.float32)] * 3 + [jax.ShapeDtypeStruct((vocab, dim), jnp.bfloat16)]
    n_el = sum(counts) * ROW_STEP * dim
    hbm, vmem = pl.BlockSpec(memory_space=pl.ANY), pl.BlockSpec(memory_space=pltpu.VMEM)
    return pl.pallas_call(
        functools.partial(adamw_kernel, counts, spots, len(extra)),
        in_specs=[vmem] + [hbm] * (3 + len(pieces) + len(extra)),
        out_specs=[hbm] * 4 + [vmem],
        out_shape=shapes + [jax.ShapeDtypeStruct((8, 128), jnp.float32)],
        scratch_shapes=[
            pltpu.VMEM((ADAMW_DEPTH, 4, ROW_STEP, dim), jnp.float32), pltpu.VMEM((ADAMW_DEPTH, 3, ROW_STEP, dim), jnp.float32),
            pltpu.VMEM((ADAMW_DEPTH, ROW_STEP, dim), jnp.bfloat16), pltpu.SemaphoreType.DMA((ADAMW_DEPTH, 4)), pltpu.SemaphoreType.DMA((ADAMW_DEPTH, 4)),
        ],
        input_output_aliases={n_in + i: i for i in range(len(extra))},
        compiler_params=pltpu.CompilerParams(vmem_limit_bytes=VMEM_LIMIT),
        cost_estimate=pl.CostEstimate(flops=ADAMW_FLOPS * n_el, bytes_accessed=30 * n_el, transcendentals=n_el),
    )(scale, *state, *pieces, *extra)


def solution(mesh):
    n_stage, n_repl, n_tp = mesh.shape["pp"], mesh.shape["dp"], mesh.shape["tp"]
    n_plane = n_stage * n_repl
    table_spec = P("tp", None)
    axes = ("tp", "dp", "pp")
    x_swap = [(i, i ^ 2) for i in range(n_stage)]
    core_swap = [(i, i ^ 1) for i in range(n_stage)]
    y_swap = [(0, 1), (1, 0)]
    corner_pairs = [(yy * n_stage + q, (1 - yy) * n_stage + q if q % 2 == 0 else yy * n_stage + (q ^ 2)) for yy in range(n_repl) for q in range(n_stage)]

    def device_step(master, exp_avg, exp_avg_sq, stage_ids, stage_acts):
        z, y, p = (lax.axis_index(a) for a in axes)
        vocab, dim = master.shape
        tok = stage_ids.shape[1] * stage_ids.shape[2]
        own_rows = -(-vocab // (n_plane * 6 * ROW_STEP)) * 6 * ROW_STEP
        plane = y * n_stage + p

        first_row = plane * own_rows
        valid = jnp.minimum(own_rows, vocab - first_row)
        scal = jnp.stack([z * vocab + first_row, valid, plane]).astype(jnp.int32)

        acts = stage_acts.reshape(tok, dim).astype(jnp.float32)
        hid, dx, all_ids = spread_call(acts, stage_ids.reshape(tok // 128, 128), n_repl)
        ids, labels = all_ids[0].reshape(1, -1), all_ids[1].reshape(1, -1)
        rows_a = own_rows // (2 * ROW_STEP) * ROW_STEP
        top_own, sum_own, hid_bf, table_a, table_b = stats_call(scal, master, (rows_a, own_rows - rows_a), hid)
        local = jnp.concatenate([top_own.reshape(-1, 128), sum_own.reshape(-1, 128)], axis=0)
        top, inv = (a.reshape(1, -1) for a in combine_call(local, float(tok)))

        n_block = own_rows // ROW_STEP
        start_b = rows_a // ROW_STEP
        part_a, sq_a = grad_call(scal, table_a, hid_bf, dx, top, inv, labels, ids, 0, tok)
        part_b, sq_b = grad_call(scal, table_b, hid_bf, dx, top, inv, labels, ids, rows_a, tok)
        scale = norm_call([sq_a, sq_b], (n_tp, n_repl, n_stage))
        part_b, scale = lax.optimization_barrier((part_b, scale))

        def across(a):
            return lax.ppermute(a, "pp", core_swap)

        def direct(a):
            from_x = lax.ppermute(a, "pp", x_swap)
            return from_x, lax.ppermute(a, "dp", y_swap)

        def corner(from_x, from_y):
            payload = jnp.where(p % 2 == 0, from_x, from_y)
            return lax.ppermute(payload, ("dp", "pp"), corner_pairs)

        def call(pieces, outs, scale):
            *outs, scale = adamw_call(scale, (master, exp_avg, exp_avg_sq), [a for a, _ in pieces], tuple(spot for _, spot in pieces), outs)
            return outs, scale

        def direct_pieces(arrays, c):
            spots = ((False, True), (True, False))
            return [(a, (*spot, False, c)) for a, spot in zip(arrays, spots)] + [(across(a), (*spot, True, c)) for a, spot in zip(arrays, spots)]

        def corner_pieces(array, c):
            return [(array, (True, True, False, c)), (across(array), (True, True, True, c))]

        def own(other_core, c):
            return (False, False, other_core, c)

        sent_a, sent_b = direct(part_a), direct(part_b)
        cross_a, cross_b = across(part_a), across(part_b)
        direct_a = direct_pieces(sent_a, 0)
        far_a = corner(*sent_a)
        outs, scale = call([(part_a, own(False, 0)), (part_b, own(False, start_b)), (cross_a, own(True, 0))], None, scale)
        outs, scale = call(direct_a + [(cross_b, own(True, start_b))], outs, scale)
        far_a, scale = lax.optimization_barrier((far_a, scale))
        outs, scale = call(corner_pieces(far_a, 0), outs, scale)
        sent_b, scale = lax.optimization_barrier((sent_b, scale))
        cut = (n_block - start_b + 1) // 2 * ROW_STEP
        far_b = [corner(*(a[:cut] for a in sent_b)), corner(*(a[cut:] for a in sent_b))]
        outs, scale = call(direct_pieces(sent_b, start_b), outs, scale)
        for i, c in enumerate((start_b, start_b + cut // ROW_STEP)):
            far, scale = lax.optimization_barrier((far_b[i], scale))
            outs, scale = call(corner_pieces(far, c), outs, scale)
        return tuple(outs)

    return jax.shard_map(device_step, mesh=mesh, in_specs=(table_spec, table_spec, table_spec, P("pp", "dp", None), P("pp", "dp", None, None)), out_specs=(table_spec, table_spec, table_spec, table_spec), check_vma=False)
```

profile of v0, /device:TPU:0, one launch (start us, length us, event | category | flops | bytes accessed | tf_op | source)
XLA Modules:
  0.0 446.5 jit_solution(4939462643566992600)
XLA Ops:
  0.7 6.8 %bitcast_convert_fusion.act_ref = f32[3072,768]{1,0:T(8,128)} fusion(bf16[1,8,384,768]{3,2,1,0:T(8,128)(2,1)} %param.9), kind=kLoop, calls=%fused_computation | loop fusion | flops 2359296 | bytes 14155776 | tf_op jit(solution)/shard_map/convert_element_type | solution.py:518
  8.1 124.6 %spread.1 = (f32[6144,768]{1,0:T(8,128)}, f32[6144,768]{1,0:T(8,128)}, s32[2,2,24,128]{3,2,1,0:T(8,128)}) custom-call(f32[3072,768]{1,0:T(8,128)} %bitcast_convert_fusion.act_ref, s32[24,128]{1,0:T(8,128)} %reshape.26.ids_ref), custom_call_target="tpu_custom_call" | custom-call | tf_op jit(solution)/shard_map/spread/pallas_call | solution.py:179
  133.4 28.0 %stats.1 = (f32[1,6144]{1,0:T(1,128)}, f32[1,6144]{1,0:T(1,128)}, bf16[6144,768]{1,0:T(8,128)(2,1)}, bf16[792,768]{1,0:T(8,128)(2,1)}, bf16[792,768]{1,0:T(8,128)(2,1)}) custom-call(s32[3]{0:T(128)} %pad_add_fusion.scal_ref, f32[12576,768]{1,0:T(8,128)} %refs_1_.11, f32[6144,768]{1,0:T(8,128)} %get-tuple-element.58.act_ref), custom_call_target="tpu_custom_call" | custom-call | flops 14948499456 | bytes 28311552 | tf_op jit(solution)/shard_map/stats/pallas_call | solution.py:272
  162.8 19.4 %combine.1 = (f32[48,128]{1,0:T(8,128)}, f32[48,128]{1,0:T(8,128)}) custom-call(f32[96,128]{1,0:T(8,128)} %pad_maximum_fusion.in_ref), custom_call_target="tpu_custom_call" | custom-call | tf_op jit(solution)/shard_map/combine/pallas_call | solution.py:233
  182.8 31.9 %shard_map.85 = (f32[792,768]{1,0:T(8,128)}, f32[1,768]{1,0:T(1,128)}) custom-call(s32[3]{0:T(128)} %pad_add_fusion.scal_ref, bf16[792,768]{1,0:T(8,128)(2,1)} %get-tuple-element.68.table_ref, bf16[6144,768]{1,0:T(8,128)(2,1)} %get-tuple-element.60.hid_ref, f32[6144,768]{1,0:T(8,128)} %get-tuple-element.61.dx_ref, f32[1,6144]{1,0:T(1,128)} %bitcast.18, ...), custom_call_target="tpu_custom_call" | custom-call | flops 22422749184 | bytes 28311552 | tf_op jit(solution)/shard_map/pallas_call | solution.py:374
  214.7 2.2 collective-permute-start.2
  217.7 31.8 %shard_map.84 = (f32[792,768]{1,0:T(8,128)}, f32[1,768]{1,0:T(1,128)}) custom-call(s32[3]{0:T(128)} %pad_add_fusion.scal_ref, bf16[792,768]{1,0:T(8,128)(2,1)} %get-tuple-element.59.table_ref, bf16[6144,768]{1,0:T(8,128)(2,1)} %get-tuple-element.60.hid_ref, f32[6144,768]{1,0:T(8,128)} %get-tuple-element.61.dx_ref, f32[1,6144]{1,0:T(1,128)} %bitcast.19, ...), custom_call_target="tpu_custom_call" | custom-call | flops 22422749184 | bytes 28311552 | tf_op jit(solution)/shard_map/pallas_call | solution.py:374
  249.5 21.5 %norm.1.refs_0_ = f32[8,128]{1,0:T(8,128)} custom-call(f32[1,768]{1,0:T(1,128)} %get-tuple-element.69.refs_0_, f32[1,768]{1,0:T(1,128)} %get-tuple-element.70.refs_1_), custom_call_target="tpu_custom_call" | custom-call | tf_op jit(solution)/shard_map/norm/pallas_call | solution.py:325
  271.7 1.8 broadcast_select_fusion
  274.2 20.4 %shard_map.86 = (f32[12576,768]{1,0:T(8,128)}, f32[12576,768]{1,0:T(8,128)}, f32[12576,768]{1,0:T(8,128)}, bf16[12576,768]{1,0:T(8,128)(2,1)}, f32[8,128]{1,0:T(8,128)}) custom-call(f32[8,128]{1,0:T(8,128)} %norm.1.refs_0_, f32[12576,768]{1,0:T(8,128)} %refs_1_.11, f32[12576,768]{1,0:T(8,128)} %refs_2_.11, f32[12576,768]{1,0:T(8,128)} %refs_3_.11, ...), custom_call_target="tpu_custom_call" | custom-call | flops 3649536000 | bytes 54743040 | tf_op jit(solution)/shard_map/pallas_call | solution.py:482
  294.7 32.2 %shard_map.87 = (f32[12576,768]{1,0:T(8,128)}, f32[12576,768]{1,0:T(8,128)}, f32[12576,768]{1,0:T(8,128)}, bf16[12576,768]{1,0:T(8,128)(2,1)}, f32[8,128]{1,0:T(8,128)}) custom-call(f32[8,128]{1,0:T(8,128)} %get-tuple-element.74.refs_0_, f32[12576,768]{1,0:T(8,128)} %refs_1_.11, ...), custom_call_target="tpu_custom_call", output_to_operand_aliasing={{0}: (9, {}), {1}: (10, {}), {2}: (11, {}), {3}: (12, {})} | custom-call | flops 6082560000 | bytes 91238400 | tf_op jit(solution)/shard_map/pallas_call | solution.py:482
  326.9 1.9 collective-permute-start.9
  328.8 1.6 collective-permute-start
  330.8 2.7 collective-permute-done.9.refs_5_
  333.4 14.5 %shard_map.88 = (f32[12576,768]{1,0:T(8,128)}, f32[12576,768]{1,0:T(8,128)}, f32[12576,768]{1,0:T(8,128)}, bf16[12576,768]{1,0:T(8,128)(2,1)}, f32[8,128]{1,0:T(8,128)}) custom-call(f32[8,128]{1,0:T(8,128)} %get-tuple-element.80.refs_0_, f32[12576,768]{1,0:T(8,128)} %refs_1_.11, ...), custom_call_target="tpu_custom_call", output_to_operand_aliasing={{0}: (6, {}), {1}: (7, {}), {2}: (8, {}), {3}: (9, {})} | custom-call | flops 2433024000 | bytes 36495360 | tf_op jit(solution)/shard_map/pallas_call | solution.py:482
  347.9 35.9 %collective-permute-done.refs_4_ = f32[792,768]{1,0:T(8,128)S(1)} collective-permute-done((f32[792,768]{1,0:T(8,128)}, f32[792,768]{1,0:T(8,128)S(1)}, u32[]{:S(2)}, u32[]{:S(2)}) %collective-permute-start) | collective-permute-done | bytes 2433056 | tf_op jit(solution)/shard_map/ppermute | solution.py:537
  385.8 2.8 slice_select_fusion
  391.3 2.0 collective-permute-done.13.refs_7_
  393.4 1.5 copy-done.3
  394.9 26.1 %shard_map.89 = (f32[12576,768]{1,0:T(8,128)}, f32[12576,768]{1,0:T(8,128)}, f32[12576,768]{1,0:T(8,128)}, bf16[12576,768]{1,0:T(8,128)(2,1)}, f32[8,128]{1,0:T(8,128)}) custom-call(f32[8,128]{1,0:T(8,128)} %get-tuple-element.89.refs_0_, f32[12576,768]{1,0:T(8,128)} %refs_1_.11, ...), custom_call_target="tpu_custom_call", output_to_operand_aliasing={{0}: (8, {}), {1}: (9, {}), {2}: (10, {}), {3}: (11, {})} | custom-call | flops 4866048000 | bytes 72990720 | tf_op jit(solution)/shard_map/pallas_call | solution.py:482
  421.2 2.6 slice_select_fusion.1
  425.7 10.4 %shard_map.90 = (f32[12576,768]{1,0:T(8,128)}, f32[12576,768]{1,0:T(8,128)}, f32[12576,768]{1,0:T(8,128)}, bf16[12576,768]{1,0:T(8,128)(2,1)}, f32[8,128]{1,0:T(8,128)}) custom-call(f32[8,128]{1,0:T(8,128)} %get-tuple-element.95.refs_0_, f32[12576,768]{1,0:T(8,128)} %refs_1_.11, ...), custom_call_target="tpu_custom_call", output_to_operand_aliasing={{0}: (6, {}), {1}: (7, {}), {2}: (8, {}), {3}: (9, {})} | custom-call | flops 1622016000 | bytes 24330240 | tf_op jit(solution)/shard_map/pallas_call | solution.py:482
  436.4 2.3 collective-permute-done.15.refs_5_
  439.6 6.7 %shard_map.91 = (f32[12576,768]{1,0:T(8,128)}, f32[12576,768]{1,0:T(8,128)}, f32[12576,768]{1,0:T(8,128)}, bf16[12576,768]{1,0:T(8,128)(2,1)}, f32[8,128]{1,0:T(8,128)}) custom-call(f32[8,128]{1,0:T(8,128)} %get-tuple-element.102.refs_0_, f32[12576,768]{1,0:T(8,128)} %refs_1_.11, ...), custom_call_target="tpu_custom_call", output_to_operand_aliasing={{0}: (6, {}), {1}: (7, {}), {2}: (8, {}), {3}: (9, {})} | custom-call | flops 811008000 | bytes 12165120 | tf_op jit(solution)/shard_map/pallas_call | solution.py:482
  (48 shorter events, 13.9 us)
Async XLA Ops:
  0.6 6.8 %copy-start.9 = (s32[1,8,384]{2,1,0:T(8,128)S(1)}, s32[1,8,384]{2,1,0:T(8,128)}, u32[]{:S(2)}) copy-start(s32[1,8,384]{2,1,0:T(8,128)} %param.8) | copy-start | bytes 36868
  133.4 48.8 %copy-start.8 = (s32[2,2,24,128]{3,2,1,0:T(8,128)S(1)}, s32[2,2,24,128]{3,2,1,0:T(8,128)}, u32[]{:S(2)}) copy-start(s32[2,2,24,128]{3,2,1,0:T(8,128)} %get-tuple-element.66) | copy-start | bytes 147460
  214.7 56.6 %collective-permute-start.2 = (f32[792,768]{1,0:T(8,128)}, f32[792,768]{1,0:T(8,128)S(1)}, u32[]{:S(2)}, u32[]{:S(2)}) collective-permute-start(f32[792,768]{1,0:T(8,128)} %get-tuple-element.72.refs_4_), channel_id=1, source_target_pairs={{0,2},{1,3},{2,0},{3,1},{4,6},{5,7},{6,4},{7,5},{8,10},{9,11},{10,... | collective-permute-start | bytes 7299080 | tf_op jit(solution)/shard_map/ppermute | solution.py:537
  216.9 54.7 %collective-permute-start.3 = (f32[792,768]{1,0:T(8,128)}, f32[792,768]{1,0:T(8,128)}, u32[]{:S(2)}, u32[]{:S(2)}) collective-permute-start(f32[792,768]{1,0:T(8,128)} %get-tuple-element.72.refs_4_), channel_id=1, source_target_pairs={{0,4},{4,0},{1,5},{5,1},{2,6},{6,2},{3,7},{7,3},{8,12},{12,8},{9,1... | collective-permute-start | bytes 7299080 | tf_op jit(solution)/shard_map/ppermute | solution.py:538
  217.7 56.5 %collective-permute-start.5 = (f32[792,768]{1,0:T(8,128)}, f32[792,768]{1,0:T(8,128)}, u32[]{:S(2)}, u32[]{:S(2)}) collective-permute-start(f32[792,768]{1,0:T(8,128)} %get-tuple-element.72.refs_4_), channel_id=1, source_target_pairs={{0,1},{1,0},{2,3},{3,2},{4,5},{5,4},{6,7},{7,6},{8,9},{9,8},{10,11... | collective-permute-start | bytes 7299080 | tf_op jit(solution)/shard_map/ppermute | solution.py:534
  271.0 23.6 %collective-permute-start.8 = (f32[792,768]{1,0:T(8,128)}, f32[792,768]{1,0:T(8,128)}, u32[]{:S(2)}, u32[]{:S(2)}) collective-permute-start(f32[792,768]{1,0:T(8,128)} %get-tuple-element.71.refs_5_), channel_id=1, source_target_pairs={{0,1},{1,0},{2,3},{3,2},{4,5},{5,4},{6,7},{7,6},{8,9},{9,8},{10,11... | collective-permute-start | bytes 7299080 | tf_op jit(solution)/shard_map/ppermute | solution.py:534
  271.2 23.4 %copy-start = (f32[792,768]{1,0:T(8,128)}, f32[792,768]{1,0:T(8,128)S(1)}, u32[]{:S(2)}) copy-start(f32[792,768]{1,0:T(8,128)S(1)} %collective-permute-done.2.refs_4_) | copy-start | bytes 7299076
  271.2 23.4 %collective-permute-start.6 = (f32[792,768]{1,0:T(8,128)S(1)}, f32[792,768]{1,0:T(8,128)}, u32[]{:S(2)}, u32[]{:S(2)}) collective-permute-start(f32[792,768]{1,0:T(8,128)S(1)} %collective-permute-done.2.refs_4_), channel_id=1, source_target_pairs={{0,1},{1,0},{2,3},{3,2},{4,5},{5,4},{6,7},{7,6},{8,9},{9,8},{10,11... | collective-permute-start | bytes 7299080 | tf_op jit(solution)/shard_map/ppermute | solution.py:534
  271.6 23.0 %collective-permute-start.7 = (f32[792,768]{1,0:T(8,128)}, f32[792,768]{1,0:T(8,128)}, u32[]{:S(2)}, u32[]{:S(2)}) collective-permute-start(f32[792,768]{1,0:T(8,128)} %collective-permute-done.3.refs_5_), channel_id=1, source_target_pairs={{0,1},{1,0},{2,3},{3,2},{4,5},{5,4},{6,7},{7,6},{8,9},{9,8},{10,11... | collective-permute-start | bytes 7299080 | tf_op jit(solution)/shard_map/ppermute | solution.py:534
  273.5 53.4 %collective-permute-start.4 = (f32[792,768]{1,0:T(8,128)}, f32[792,768]{1,0:T(8,128)}, u32[]{:S(2)}, u32[]{:S(2)}) collective-permute-start(f32[792,768]{1,0:T(8,128)} %broadcast_select_fusion), channel_id=1, source_target_pairs={{0,4},{1,3},{2,6},{3,1},{4,0},{5,7},{6,2},{7,5},{8,12},{9,11},{10,... | collective-permute-start | bytes 7299080 | tf_op jit(solution)/shard_map/ppermute | solution.py:542
  326.9 6.5 %collective-permute-start.9 = (f32[792,768]{1,0:T(8,128)}, f32[792,768]{1,0:T(8,128)}, u32[]{:S(2)}, u32[]{:S(2)}) collective-permute-start(f32[792,768]{1,0:T(8,128)} %collective-permute-done.4.refs_4_), channel_id=1, source_target_pairs={{0,1},{1,0},{2,3},{3,2},{4,5},{5,4},{6,7},{7,6},{8,9},{9,8},{10,11... | collective-permute-start | bytes 7299080 | tf_op jit(solution)/shard_map/ppermute | solution.py:534
  328.8 55.0 %collective-permute-start = (f32[792,768]{1,0:T(8,128)}, f32[792,768]{1,0:T(8,128)S(1)}, u32[]{:S(2)}, u32[]{:S(2)}) collective-permute-start(f32[792,768]{1,0:T(8,128)} %get-tuple-element.71.refs_5_), channel_id=1, source_target_pairs={{0,2},{1,3},{2,0},{3,1},{4,6},{5,7},{6,4},{7,5},{8,10},{9,11},{10,... | collective-permute-start | bytes 7299080 | tf_op jit(solution)/shard_map/ppermute | solution.py:537
  330.4 54.8 %collective-permute-start.1 = (f32[792,768]{1,0:T(8,128)}, f32[792,768]{1,0:T(8,128)}, u32[]{:S(2)}, u32[]{:S(2)}) collective-permute-start(f32[792,768]{1,0:T(8,128)} %get-tuple-element.71.refs_5_), channel_id=1, source_target_pairs={{0,4},{4,0},{1,5},{5,1},{2,6},{6,2},{3,7},{7,3},{8,12},{12,8},{9,1... | collective-permute-start | bytes 7299080 | tf_op jit(solution)/shard_map/ppermute | solution.py:538
  383.8 11.0 %copy-start.1 = (f32[792,768]{1,0:T(8,128)}, f32[792,768]{1,0:T(8,128)S(1)}, u32[]{:S(2)}) copy-start(f32[792,768]{1,0:T(8,128)S(1)} %collective-permute-done.refs_4_) | copy-start | bytes 7299076
  385.2 4.6 %collective-permute-start.12 = (f32[792,768]{1,0:T(8,128)S(1)}, f32[792,768]{1,0:T(8,128)S(1)}, u32[]{:S(2)}, u32[]{:S(2)}) collective-permute-start(f32[792,768]{1,0:T(8,128)S(1)} %collective-permute-done.refs_4_), channel_id=1, source_target_pairs={{0,1},{1,0},{2,3},{3,2},{4,5},{5,4},{6,7},{7,6},{8,9},{9,8},{10,11... | collective-permute-start | bytes 7299080 | tf_op jit(solution)/shard_map/ppermute | solution.py:534
  385.3 8.1 %collective-permute-start.13 = (f32[792,768]{1,0:T(8,128)}, f32[792,768]{1,0:T(8,128)S(1)}, u32[]{:S(2)}, u32[]{:S(2)}) collective-permute-start(f32[792,768]{1,0:T(8,128)} %collective-permute-done.1.refs_5_), channel_id=1, source_target_pairs={{0,1},{1,0},{2,3},{3,2},{4,5},{5,4},{6,7},{7,6},{8,9},{9,8},{10,11... | collective-permute-start | bytes 7299080 | tf_op jit(solution)/shard_map/ppermute | solution.py:534
  388.5 32.4 %collective-permute-start.11 = (f32[528,768]{1,0:T(8,128)}, f32[528,768]{1,0:T(8,128)S(1)}, u32[]{:S(2)}, u32[]{:S(2)}) collective-permute-start(f32[528,768]{1,0:T(8,128)} %slice_select_fusion), channel_id=1, source_target_pairs={{0,4},{1,3},{2,6},{3,1},{4,0},{5,7},{6,2},{7,5},{8,12},{9,11},{10,... | collective-permute-start | bytes 4866056 | tf_op jit(solution)/shard_map/ppermute | solution.py:542
  389.9 1.4 copy-start.2
  393.4 1.5 copy-start.3
  420.9 3.6 copy-start.4
  420.9 3.5 collective-permute-start.14
  423.9 12.5 %collective-permute-start.10 = (f32[264,768]{1,0:T(8,128)}, f32[264,768]{1,0:T(8,128)S(1)}, u32[]{:S(2)}, u32[]{:S(2)}) collective-permute-start(f32[264,768]{1,0:T(8,128)} %slice_select_fusion.1), channel_id=1, source_target_pairs={{0,4},{1,3},{2,6},{3,1},{4,0},{5,7},{6,2},{7,5},{8,12},{9,11},{10,... | collective-permute-start | bytes 2433032 | tf_op jit(solution)/shard_map/ppermute | solution.py:542
  436.3 2.3 copy-start.6
  436.3 2.3 collective-permute-start.15
  (2 other events, 2.1 us)
where the time goes:
time: 447 us; the launch traced here: 446 us
  Pallas kernels  367 us (82%)
  waiting for transfers between devices  45.5 us (10%)
  other arithmetic  16 us (4%)
  starting transfers between devices  10.2 us (2%)
  local copies, waits for them, and re-layouts  6.27 us (1%)
    pallas_call x1, Pallas kernels, spread_call(): pl.pallas_call(spread_kernel, in_specs=[pl.BlockSpec(memory_space=pl.ANY)...  125 us
    pallas_call x6, Pallas kernels, adamw_call(): pl.pallas_call(functools.partial(adamw_kernel, counts, spots, len(extra))...  110 us
    pallas_call x2, Pallas kernels, grad_call(): pl.pallas_call(functools.partial(grad_kernel, offset, tok_count), grid=(t...  63.7 us
    ppermute x2, waiting for transfers between devices, direct(): from_x = lax.ppermute(a, 'pp', x_swap)  35.9 us
    pallas_call x1, Pallas kernels, stats_call(): pl.pallas_call(stats_kernel, grid_spec=pltpu.PrefetchScalarGridSpec(num_s...  28 us
    pallas_call x1, Pallas kernels, norm_call(): pl.pallas_call(functools.partial(norm_kernel, n_dev), in_specs=[vmem] * l...  21.5 us
    pallas_call x1, Pallas kernels, combine_call(): pl.pallas_call(functools.partial(combine_kernel, scale), in_specs=[pl.Blo...  19.4 us
  transfers between devices with their start and end apart: 16, of which 8 were waited for; matrix products, arithmetic and copies ran while one was open for 2% of the time, Pallas kernels for 35%

commit v1 on v0

--- a/solution.py
+++ b/solution.py
@@ -31,164 +31,250 @@
 MESH = pl.DeviceIdType.MESH
 
 
-def spread_kernel(act_ref, ids_ref, hid_ref, look_ref, all_ids_ref, buf, ids_buf, sx, sy, sz, sd, sl, si, load, recv, recv_core, recv_ids):
+def spread_kernel(rows_valid, act_ref, ids_ref, master_ref, hid_ref, look_ref, all_ids_ref, table_ref, top_ref, sum_ref,
+                  buf, hid_buf, master_buf, ids_buf, sx, sy, sz, sd, sl, so, si, load, sm, recv, recv_core, recv_ids):
     z, y, p = lax.axis_index("tp"), lax.axis_index("dp"), lax.axis_index("pp")
     x, core, odd = p // 2, p % 2, z % 2
+    is_src = x == core
     x_dev = {"pp": (1 - x) * 2 + core}
     y_dev = {"dp": 1 - y}
     z_dev = {"tp": z + 1 - 2 * odd}
     core_dev = {"pp": x * 2 + 1 - core}
     plane = [{"dp": (y + dy) % 2, "pp": (p + dp) % 4} for dy in range(2) for dp in range(4) if dy + dp > 0]
     n = SPREAD_CHUNKS
-    edge, main = n // 3, 2 * n // 3
+    edge, main, lag, unit = n // 3, 2 * n // 3, 3, 4
     tok = act_ref.shape[0]
     size = tok // n
-
-    barrier = pltpu.get_barrier_semaphore()
-    for dev in plane + [z_dev]:
-        pl.semaphore_signal(barrier, inc=1, device_id=dev, device_id_type=MESH)
-    pl.semaphore_wait(barrier, len(plane) + 1)
+    rows = table_ref.shape[0]
+    device = y * 4 + p
+    last = len(plane)
+    meet(plane + [z_dev])
 
     def chunk(i):
         if i < edge:
             return odd * main + i
         return i if i < main else (1 - odd) * main + (i - main)
 
-    def span(replica, i):
-        return pl.ds(pl.multiple_of(replica * tok + chunk(i) * size, size), size)
+    def span(slot, i, count=1):
+        replica = y if slot == 0 else 1 - y
+        return pl.ds(pl.multiple_of(replica * tok + chunk(i) * size, size), size * count)
 
     def remote(src, dst, send_sem, recv_sem, dev):
-        copy = pltpu.make_async_remote_copy(src_ref=src, dst_ref=dst, send_sem=send_sem, recv_sem=recv_sem, device_id=dev, device_id_type=MESH)
-        copy.start()
-        return copy
+        pltpu.make_async_remote_copy(src_ref=src, dst_ref=dst, send_sem=send_sem, recv_sem=recv_sem, device_id=dev, device_id_type=MESH).start()
+
+    def send(slot, i, send_sem, recv_sem, dev):
+        view = buf.at[core, span(slot, i)]
+        remote(view, view, send_sem, recv_sem, dev)
+
+    def drain(sem):
+        view = buf.at[0, pl.ds(0, size)]
+        pltpu.make_async_copy(view, view, sem).wait()
+
+    def arrived(slot, i):
+        drain(recv.at[slot, i])
+
+    def keep(slot, i):
+        send(slot, i, sd.at[slot, i], recv_core.at[slot, i], core_dev)
 
     def send_ids(kind):
-        local = pltpu.make_async_copy(ids_ref, ids_buf.at[kind, y], recv_ids.at[kind, y])
-        local.start()
+        pltpu.make_async_copy(ids_ref, ids_buf.at[kind, y], recv_ids.at[kind, y]).start()
         for i, dev in enumerate(plane):
             remote(ids_ref, ids_buf.at[kind, y], si.at[i], recv_ids.at[kind, y], dev)
 
-    def drain_ids():
-        for i in range(len(plane)):
-            pltpu.make_async_copy(ids_ref, ids_ref, si.at[i]).wait()
-
     pl.when(p == 0)(lambda: send_ids(0))
     pl.when(p == 3)(lambda: send_ids(1))
 
-    def run(out_ref, x_src):
-
-        def send(replica, i, send_sem, recv_sem, dev):
-            view = buf.at[span(replica, i)]
-            return remote(view, view, send_sem, recv_sem, dev)
-
-        def arrived(replica, i, slot):
-            view = buf.at[span(replica, i)]
-            pltpu.make_async_copy(view, view, recv.at[slot, i]).wait()
-
-        def keep(copies, replica, i, slot):
-            view, place = buf.at[span(replica, i)], out_ref.at[span(replica, i)]
-            copies.append(remote(view, place, sd.at[slot, i], recv_core.at[slot, i], core_dev).wait_send)
-            local = pltpu.make_async_copy(view, place, sl.at[slot, i])
-            local.start()
-            copies.append(local.wait)
-
-        @pl.when(x == x_src)
+    def master_copy(count):
+        return pltpu.make_async_copy(master_ref.at[pl.ds(pl.multiple_of(device * rows, 8), count)], master_buf.at[pl.ds(0, count)], sm.at[0])
+
+    pl.when(device < last)(lambda: master_copy(rows).start())
+
+    @pl.when(device == last)
+    def _():
+        master_copy(rows_valid).start()
+        if rows_valid < rows:
+            master_buf[rows_valid:, :] = jnp.zeros((rows - rows_valid, master_buf.shape[1]), jnp.float32)
+
+    @pl.when(is_src)
+    def _():
+        def load_copy(i):
+            place = pl.ds(pl.multiple_of(chunk(i) * size, size), size)
+            return pltpu.make_async_copy(act_ref.at[place], buf.at[core, span(0, i)], load.at[i])
+
+        for i in range(n):
+            load_copy(i).start()
+        for i in range(n):
+            load_copy(i).wait()
+            if i < edge:
+                send(0, i, sx.at[i], recv.at[0, i], x_dev)
+            if i < main:
+                send(0, i, sy.at[i], recv.at[1, i], y_dev)
+        for i in range(n):
+            keep(0, i)
+
+    pl.when(device < last)(lambda: master_copy(rows).wait())
+    pl.when(device == last)(lambda: master_copy(rows_valid).wait())
+    table_ref[...] = master_buf[...].astype(jnp.bfloat16)
+    valid = jnp.where(device == last, rows_valid, rows)
+
+    def statistics(slot, i):
+        place = span(slot, i, unit)
+        act = buf[1, place, :].astype(jnp.bfloat16)
+        hid_buf[place, :] = act
+        pltpu.make_async_copy(hid_buf.at[place], hid_ref.at[place], so.at[slot, i // unit]).start()
+
+        def tile(r, carry):
+            top, total = carry
+            start = pl.multiple_of(r * ROW_STEP, 8)
+            logits = dot_nt(table_ref[pl.ds(start, ROW_STEP), :], act)
+            row = start + lax.broadcasted_iota(jnp.int32, logits.shape, 0)
+            logits = jnp.where(row < valid, logits, -jnp.inf)
+            new_top = jnp.maximum(top, jnp.max(logits, axis=0, keepdims=True))
+            return new_top, total * jnp.exp(top - new_top) + jnp.sum(jnp.exp(logits - new_top), axis=0, keepdims=True)
+
+        empty = jnp.full((1, size * unit), -jnp.inf, jnp.float32)
+        top, total = lax.fori_loop(0, rows // ROW_STEP, tile, (empty, jnp.zeros_like(empty)))
+        where = pl.ds((y if slot == 0 else 1 - y) * (n // unit) + chunk(i) // unit, 1)
+        top_ref[where, :] = top
+        sum_ref[where, :] = total
+
+    def ready(slot, i):
+        drain(recv_core.at[slot, i])
+        place = span(slot, i)
+        pltpu.make_async_copy(buf.at[0, place], look_ref.at[place], sl.at[slot, i]).start()
+        if i % unit == unit - 1:
+            statistics(slot, i - unit + 1)
+
+    def source_step(s):
+        arrived(1, s)
+        if s + edge < main:
+            send(0, s + edge, sx.at[s + edge], recv.at[0, s + edge], x_dev)
+        if s % 2 == 0:
+            send(1, s, sx.at[main + s // 2], recv.at[1, s], x_dev)
+        if s < edge:
+            send(1, s, sz.at[1, s], recv.at[1, main + s], z_dev)
+        keep(1, s)
+
+    def other_step(s):
+        if s < main:
+            arrived(0, s)
+            if s % 2 == 1:
+                send(0, s, sy.at[s], recv.at[1, s], y_dev)
+            if s < edge:
+                send(0, s, sz.at[0, s], recv.at[0, main + s], z_dev)
+            keep(0, s)
+        i = s - edge
+        if i >= 0:
+            arrived(1, i)
+            if i < edge:
+                send(1, i, sz.at[1, i], recv.at[1, main + i], z_dev)
+            keep(1, i)
+
+    def take_far(slot, i):
+        arrived(slot, i)
+        keep(slot, i)
+
+    done = set()
+
+    def ready_once(slot, i):
+        if 0 <= i and (slot, i) not in done:
+            done.add((slot, i))
+            ready(slot, i)
+
+    for s in range(main + edge):
+        far = main + (s - 4) // 2 if s >= 4 and s % 2 == 0 and (s - 4) // 2 < edge else None
+
+        @pl.when(is_src)
         def _():
-            copies, loads = [], []
-            for i in range(n):
-                rows = pl.ds(pl.multiple_of(chunk(i) * size, size), size)
-                loads.append(pltpu.make_async_copy(act_ref.at[rows], buf.at[span(y, i)], load.at[i]))
-                loads[-1].start()
-            for i in range(n):
-                loads[i].wait()
-                if i < edge:
-                    copies.append(send(y, i, sx.at[i], recv.at[0, i], x_dev).wait_send)
-                if i < main:
-                    copies.append(send(y, i, sy.at[i], recv.at[1, i], y_dev).wait_send)
-            for i in range(n):
-                keep(copies, y, i, 0)
-            for i in range(main):
-                arrived(1 - y, i, 1)
-                if i + edge < main:
-                    copies.append(send(y, i + edge, sx.at[i + edge], recv.at[0, i + edge], x_dev).wait_send)
-                if i % 2 == 0:
-                    copies.append(send(1 - y, i, sx.at[main + i // 2], recv.at[1, i], x_dev).wait_send)
-                if i < edge:
-                    copies.append(send(1 - y, i, sz.at[1, i], recv.at[1, main + i], z_dev).wait_send)
-                keep(copies, 1 - y, i, 1)
-            for i in range(main, n):
-                arrived(1 - y, i, 1)
-                keep(copies, 1 - y, i, 1)
-            for wait in copies:
-                wait()
-
-        @pl.when(x != x_src)
+            if s < main:
+                source_step(s)
+            if far is not None:
+                take_far(1, far)
+
+        @pl.when(jnp.logical_not(is_src))
         def _():
-            copies = []
-            for s in range(main + edge):
-                if s < main:
-                    arrived(y, s, 0)
-                    if s % 2 == 1:
-                        copies.append(send(y, s, sy.at[s], recv.at[1, s], y_dev).wait_send)
-                    if s < edge:
-                        copies.append(send(y, s, sz.at[0, s], recv.at[0, main + s], z_dev).wait_send)
-                    keep(copies, y, s, 0)
-                if s >= edge:
-                    i = s - edge
-                    arrived(1 - y, i, 1)
-                    if i < edge:
-                        copies.append(send(1 - y, i, sz.at[1, i], recv.at[1, main + i], z_dev).wait_send)
-                    keep(copies, 1 - y, i, 1)
-            for i in range(main, n):
-                for slot, replica in ((0, y), (1, 1 - y)):
-                    arrived(replica, i, slot)
-                    keep(copies, replica, i, slot)
-            for wait in copies:
-                wait()
-
-    def wait_core(out_ref):
-        for slot, replica in ((0, y), (1, 1 - y)):
-            for i in range(n):
-                view = out_ref.at[span(replica, i)]
-                pltpu.make_async_copy(view, view, recv_core.at[slot, i]).wait()
-
-    @pl.when(core == 1)
-    def _():
-        run(hid_ref, 1)
-        wait_core(look_ref)
-
-    @pl.when(core == 0)
-    def _():
-        run(look_ref, 0)
-        wait_core(hid_ref)
+            other_step(s)
+            if far is not None:
+                take_far(0, far)
+
+        if s - lag < main:
+            ready_once(0, s - lag)
+        if s - edge - lag < main:
+            ready_once(1, s - edge - lag)
+        j = s - 4 - lag
+        if j >= 0 and j % 2 == 0 and j // 2 < edge:
+            ready_once(0, main + j // 2)
+
+    @pl.when(jnp.logical_not(is_src))
+    def _():
+        for i in range(main, n):
+            take_far(1, i)
+
+    for slot in range(2):
+        for i in range(n):
+            ready_once(slot, i)
+
+    for i in range(main):
+        if i % 2 == 1:
+            drain(sy.at[i])
+    for i in range(edge):
+        drain(sz.at[1, i])
+    for slot in range(2):
+        for i in range(n):
+            drain(sd.at[slot, i])
+            drain(sl.at[slot, i])
+        for i in range(n // unit):
+            view = hid_buf.at[pl.ds(0, size * unit)]
+            pltpu.make_async_copy(view, view, so.at[slot, i]).wait()
+
+    @pl.when(is_src)
+    def _():
+        for i in range(main + main // 2):
+            drain(sx.at[i])
+        for i in range(0, main, 2):
+            drain(sy.at[i])
+
+    @pl.when(jnp.logical_not(is_src))
+    def _():
+        for i in range(edge):
+            drain(sz.at[0, i])
 
     for kind in range(2):
         for replica in range(2):
             pltpu.make_async_copy(ids_ref, ids_buf.at[kind, replica], recv_ids.at[kind, replica]).wait()
-    pl.when(p == 0)(drain_ids)
-    pl.when(p == 3)(drain_ids)
+
+    @pl.when(jnp.logical_or(p == 0, p == 3))
+    def _():
+        for i in range(len(plane)):
+            pltpu.make_async_copy(ids_ref, ids_ref, si.at[i]).wait()
+
     all_ids_ref[...] = ids_buf[...]
 
 
-def spread_call(acts, ids, n_repl):
+def spread_call(acts, ids, master, rows, n_repl):
     tok, dim = acts.shape
-    n = SPREAD_CHUNKS
-    shape = jax.ShapeDtypeStruct((n_repl * tok, dim), jnp.float32)
+    n, unit = SPREAD_CHUNKS, 4
     ids_shape = (2, n_repl) + ids.shape
     dma = pltpu.SemaphoreType.DMA
+    hbm, vmem = pl.BlockSpec(memory_space=pl.ANY), pl.BlockSpec(memory_space=pltpu.VMEM)
+    stat = jax.ShapeDtypeStruct((n_repl * n // unit, tok // n * unit), jnp.float32)
     return pl.pallas_call(
-        spread_kernel,
-        in_specs=[pl.BlockSpec(memory_space=pl.ANY), pl.BlockSpec(memory_space=pltpu.VMEM)],
-        out_specs=[pl.BlockSpec(memory_space=pl.ANY)] * 2 + [pl.BlockSpec(memory_space=pltpu.VMEM)],
-        out_shape=[shape, shape, jax.ShapeDtypeStruct(ids_shape, jnp.int32)],
+        functools.partial(spread_kernel, master.shape[0] - 7 * rows),
+        in_specs=[hbm, vmem, hbm],
+        out_specs=[hbm, hbm, vmem, vmem, vmem, vmem],
+        out_shape=[
+            jax.ShapeDtypeStruct((n_repl * tok, dim), jnp.bfloat16), jax.ShapeDtypeStruct((n_repl * tok, dim), jnp.float32),
+            jax.ShapeDtypeStruct(ids_shape, jnp.int32), jax.ShapeDtypeStruct((rows, dim), jnp.bfloat16), stat, stat,
+        ],
         scratch_shapes=[
-            pltpu.VMEM((n_repl * tok, dim), jnp.float32), pltpu.VMEM(ids_shape, jnp.int32),
-            dma((n + n // 2,)), dma((n,)), dma((2, n // 3)), dma((2, n)), dma((2, n)), dma((8,)),
-            dma((n,)), dma((2, n)), dma((2, n)), dma((2, 2)),
+            pltpu.VMEM((2, n_repl * tok, dim), jnp.float32), pltpu.VMEM((n_repl * tok, dim), jnp.bfloat16), pltpu.VMEM((rows, dim), jnp.float32),
+            pltpu.VMEM(ids_shape, jnp.int32),
+            dma((n + n // 2,)), dma((n,)), dma((2, n // 3)), dma((2, n)), dma((2, n)), dma((2, n // unit)), dma((8,)),
+            dma((n,)), dma((1,)), dma((2, n)), dma((2, n)), dma((2, 2)),
         ],
         compiler_params=pltpu.CompilerParams(collective_id=0, has_side_effects=True, vmem_limit_bytes=VMEM_LIMIT),
         name="spread",
-    )(acts, ids)
+    )(acts, ids, master)
 
 
 def slice_partners(z, y, p):
@@ -239,60 +325,6 @@
         compiler_params=pltpu.CompilerParams(collective_id=1, has_side_effects=True),
         name="combine",
     )(local)
-
-
-def stats_kernel(scal_ref, master_ref, act_ref, max_ref, sum_ref, cast_ref, *table_refs):
-    @pl.when(pl.program_id(0) == 0)
-    def _():
-        start = 0
-        for ref in table_refs:
-            ref[...] = master_ref[start:start + ref.shape[0], :].astype(jnp.bfloat16)
-            start += ref.shape[0]
-
-    act = act_ref[...].astype(jnp.bfloat16)
-    cast_ref[...] = act
-    rows = master_ref.shape[0]
-    tiles = [ref[i:i + ROW_STEP, :] for ref in table_refs for i in range(0, ref.shape[0], ROW_STEP)]
-    parts = []
-    for start, tile in zip(range(0, rows, ROW_STEP), tiles):
-        logits = dot_nt(tile, act)
-        if start + ROW_STEP == rows:
-            row = start + lax.broadcasted_iota(jnp.int32, logits.shape, 0)
-            logits = jnp.where(row < scal_ref[1], logits, -jnp.inf)
-        top = jnp.max(logits, axis=0, keepdims=True)
-        parts.append((top, jnp.sum(jnp.exp(logits - top), axis=0, keepdims=True)))
-    top_all = functools.reduce(jnp.maximum, [p[0] for p in parts])
-    max_ref[...] = top_all
-    sum_ref[...] = functools.reduce(jnp.add, [p[1] * jnp.exp(p[0] - top_all) for p in parts])
-
-
-def stats_call(scal, master, splits, acts):
-    tokens, dim = acts.shape
-    rows = sum(splits)
-    return pl.pallas_call(
-        stats_kernel,
-        grid_spec=pltpu.PrefetchScalarGridSpec(
-            num_scalar_prefetch=1,
-            grid=(tokens // TOK_STEP,),
-            in_specs=[
-                pl.BlockSpec((rows, dim), lambda t, scal: (scal[2], 0), pipeline_mode=pl.Buffered(1)),
-                pl.BlockSpec((TOK_STEP, dim), lambda t, scal: (t, 0)),
-            ],
-            out_specs=[
-                pl.BlockSpec((1, TOK_STEP), lambda t, scal: (0, t)),
-                pl.BlockSpec((1, TOK_STEP), lambda t, scal: (0, t)),
-                pl.BlockSpec((TOK_STEP, dim), lambda t, scal: (t, 0)),
-            ] + [pl.BlockSpec((part, dim), lambda t, scal: (0, 0)) for part in splits],
-        ),
-        out_shape=[
-            jax.ShapeDtypeStruct((1, tokens), jnp.float32),
-            jax.ShapeDtypeStruct((1, tokens), jnp.float32),
-            jax.ShapeDtypeStruct((tokens, dim), jnp.bfloat16),
-        ] + [jax.ShapeDtypeStruct((part, dim), jnp.bfloat16) for part in splits],
-        compiler_params=pltpu.CompilerParams(vmem_limit_bytes=VMEM_LIMIT),
-        cost_estimate=pl.CostEstimate(flops=2 * tokens * rows * dim, bytes_accessed=6 * tokens * dim, transcendentals=tokens * rows),
-        name="stats",
-    )(scal, master, acts)
 
 
 def norm_kernel(n_dev, *refs):
@@ -368,7 +400,8 @@
 
 def grad_call(scal, table_bf, hid, dx, top, inv, labels, ids, offset, tok_count):
     tokens, dim = hid.shape
-    rows, n_out = table_bf.shape[0], 1
+    rows, n_out = table_bf.shape[0] // 2, 1
+    half = offset // rows
     tok_spec = pl.BlockSpec((1, TOK_STEP), lambda t: (0, t))
     act_spec = pl.BlockSpec((TOK_STEP, dim), lambda t: (t, 0))
     return pl.pallas_call(
@@ -376,7 +409,7 @@
         grid=(tokens // TOK_STEP,),
         in_specs=[
             pl.BlockSpec(memory_space=pltpu.SMEM),
-            pl.BlockSpec((rows * n_out, dim), lambda t: (0, 0)),
+            pl.BlockSpec((rows * n_out, dim), lambda t: (half, 0)),
             act_spec, act_spec, tok_spec, tok_spec, tok_spec, tok_spec,
         ],
         out_specs=[pl.BlockSpec((rows, dim), lambda t: (0, 0))] * n_out + [pl.BlockSpec((1, dim), lambda t: (0, 0))],
@@ -513,20 +546,19 @@
 
         first_row = plane * own_rows
         valid = jnp.minimum(own_rows, vocab - first_row)
-        scal = jnp.stack([z * vocab + first_row, valid, plane]).astype(jnp.int32)
+        scal = jnp.stack([z * vocab + first_row, valid]).astype(jnp.int32)
 
         acts = stage_acts.reshape(tok, dim).astype(jnp.float32)
-        hid, dx, all_ids = spread_call(acts, stage_ids.reshape(tok // 128, 128), n_repl)
+        hid_bf, dx, all_ids, table_bf, top_own, sum_own = spread_call(acts, stage_ids.reshape(tok // 128, 128), master, own_rows, n_repl)
         ids, labels = all_ids[0].reshape(1, -1), all_ids[1].reshape(1, -1)
         rows_a = own_rows // (2 * ROW_STEP) * ROW_STEP
-        top_own, sum_own, hid_bf, table_a, table_b = stats_call(scal, master, (rows_a, own_rows - rows_a), hid)
         local = jnp.concatenate([top_own.reshape(-1, 128), sum_own.reshape(-1, 128)], axis=0)
         top, inv = (a.reshape(1, -1) for a in combine_call(local, float(tok)))
 
         n_block = own_rows // ROW_STEP
         start_b = rows_a // ROW_STEP
-        part_a, sq_a = grad_call(scal, table_a, hid_bf, dx, top, inv, labels, ids, 0, tok)
-        part_b, sq_b = grad_call(scal, table_b, hid_bf, dx, top, inv, labels, ids, rows_a, tok)
+        part_a, sq_a = grad_call(scal, table_bf, hid_bf, dx, top, inv, labels, ids, 0, tok)
+        part_b, sq_b = grad_call(scal, table_bf, hid_bf, dx, top, inv, labels, ids, rows_a, tok)
         scale = norm_call([sq_a, sq_b], (n_tp, n_repl, n_stage))
         part_b, scale = lax.optimization_barrier((part_b, scale))
 

time: 447 us -> 435 us (0.973)
  Pallas kernels: 367 us -> 355 us
    pallas_call x2 -> x1, Pallas kernels: 153 us -> 140 us  [spread_call(): pl.pallas_call(functools.partial(spread_kernel, master.shape[0] - 7 * row...]
  transfers between devices with their start and end apart: 16 -> 16, of which waited for: 8 -> 5; matrix products, arithmetic and copies ran while one was open for 2% -> 2% of each run, Pallas kernels for 35% -> 36%
where the time goes in v1:
time: 435 us; the launch traced here: 434 us
  Pallas kernels  355 us (82%)
  waiting for transfers between devices  42.9 us (10%)
  other arithmetic  15.5 us (4%)
  starting transfers between devices  11.8 us (3%)
  local copies, waits for them, and re-layouts  8.59 us (2%)
    pallas_call x1, Pallas kernels, spread_call(): pl.pallas_call(functools.partial(spread_kernel, master.shape[0] - 7 * row...  140 us
    pallas_call x6, Pallas kernels, adamw_call(): pl.pallas_call(functools.partial(adamw_kernel, counts, spots, len(extra))...  110 us
    pallas_call x2, Pallas kernels, grad_call(): pl.pallas_call(functools.partial(grad_kernel, offset, tok_count), grid=(t...  63.6 us
    ppermute x2, waiting for transfers between devices, direct(): from_x = lax.ppermute(a, 'pp', x_swap)  35.8 us
    pallas_call x1, Pallas kernels, norm_call(): pl.pallas_call(functools.partial(norm_kernel, n_dev), in_specs=[vmem] * l...  20.9 us
    pallas_call x1, Pallas kernels, combine_call(): pl.pallas_call(functools.partial(combine_kernel, scale), in_specs=[pl.Blo...  19.3 us
  transfers between devices with their start and end apart: 16, of which 5 were waited for; matrix products, arithmetic and copies ran while one was open for 2% of the time, Pallas kernels for 36%

profile of v1, /device:TPU:0, one launch (start us, length us, event | category | flops | bytes accessed | tf_op | source)
XLA Modules:
  0.0 434.3 jit_solution(16686896528518053254)
XLA Ops:
  0.7 6.8 %bitcast_convert_fusion.act_ref = f32[3072,768]{1,0:T(8,128)} fusion(bf16[1,8,384,768]{3,2,1,0:T(8,128)(2,1)} %param.9), kind=kLoop, calls=%fused_computation | loop fusion | flops 2359296 | bytes 14155776 | tf_op jit(solution)/shard_map/convert_element_type | solution.py:551
  8.1 140.4 %spread.1 = (bf16[6144,768]{1,0:T(8,128)(2,1)}, f32[6144,768]{1,0:T(8,128)}, s32[2,2,24,128]{3,2,1,0:T(8,128)}, bf16[1584,768]{1,0:T(8,128)(2,1)}, f32[12,512]{1,0:T(8,128)}, /*index=5*/f32[12,512]{1,0:T(8,128)}) custom-call(f32[3072,768]{1,0:T(8,128)} %bitcast_convert_fusion.act_ref, s32[24,128]{1,0:T(8,128)} %reshape.26.ids_ref, f32[12576,768]{1,0:T(8,128)} %refs_1_.11), custom_call_target="tpu_custom_call" | custom-call | tf_op jit(solution)/shard_map/spread/pallas_call | solution.py:261
  150.7 19.3 %combine.1 = (f32[48,128]{1,0:T(8,128)}, f32[48,128]{1,0:T(8,128)}) custom-call(f32[96,128]{1,0:T(8,128)} %pad_maximum_fusion.in_ref), custom_call_target="tpu_custom_call" | custom-call | tf_op jit(solution)/shard_map/combine/pallas_call | solution.py:319
  172.0 31.8 %shard_map.85 = (f32[792,768]{1,0:T(8,128)}, f32[1,768]{1,0:T(1,128)}) custom-call(s32[2]{0:T(128)} %pad_add_fusion.scal_ref, bf16[1584,768]{1,0:T(8,128)(2,1)} %get-tuple-element.56.table_ref, bf16[6144,768]{1,0:T(8,128)(2,1)} %get-tuple-element.57.hid_ref, f32[6144,768]{1,0:T(8,128)} %get-tuple-element.58.dx_ref, f32[1,6144]{1,0:T(1,128)} %bitcast.13, ...), custom_call_target="tpu_custom_call" | custom-call | flops 22422749184 | bytes 28311552 | tf_op jit(solution)/shard_map/pallas_call | solution.py:407
  203.8 1.8 collective-permute-start.3
  205.5 31.8 %shard_map.84 = (f32[792,768]{1,0:T(8,128)}, f32[1,768]{1,0:T(1,128)}) custom-call(s32[2]{0:T(128)} %pad_add_fusion.scal_ref, bf16[1584,768]{1,0:T(8,128)(2,1)} %get-tuple-element.56.table_ref, bf16[6144,768]{1,0:T(8,128)(2,1)} %get-tuple-element.57.hid_ref, f32[6144,768]{1,0:T(8,128)} %get-tuple-element.58.dx_ref, f32[1,6144]{1,0:T(1,128)} %bitcast.14, ...), custom_call_target="tpu_custom_call" | custom-call | flops 22422749184 | bytes 28311552 | tf_op jit(solution)/shard_map/pallas_call | solution.py:407
  237.4 20.9 %norm.1.refs_0_ = f32[8,128]{1,0:T(8,128)} custom-call(f32[1,768]{1,0:T(1,128)} %get-tuple-element.65.refs_0_, f32[1,768]{1,0:T(1,128)} %get-tuple-element.66.refs_1_), custom_call_target="tpu_custom_call" | custom-call | tf_op jit(solution)/shard_map/norm/pallas_call | solution.py:357
  259.0 1.8 broadcast_select_fusion
  260.7 1.8 collective-permute-start.4
  262.5 20.4 %shard_map.86 = (f32[12576,768]{1,0:T(8,128)}, f32[12576,768]{1,0:T(8,128)}, f32[12576,768]{1,0:T(8,128)}, bf16[12576,768]{1,0:T(8,128)(2,1)}, f32[8,128]{1,0:T(8,128)}) custom-call(f32[8,128]{1,0:T(8,128)} %norm.1.refs_0_, f32[12576,768]{1,0:T(8,128)} %refs_1_.11, f32[12576,768]{1,0:T(8,128)} %refs_2_.11, f32[12576,768]{1,0:T(8,128)} %refs_3_.11, ...), custom_call_target="tpu_custom_call" | custom-call | flops 3649536000 | bytes 54743040 | tf_op jit(solution)/shard_map/pallas_call | solution.py:515
  283.0 32.2 %shard_map.87 = (f32[12576,768]{1,0:T(8,128)}, f32[12576,768]{1,0:T(8,128)}, f32[12576,768]{1,0:T(8,128)}, bf16[12576,768]{1,0:T(8,128)(2,1)}, f32[8,128]{1,0:T(8,128)}) custom-call(f32[8,128]{1,0:T(8,128)} %get-tuple-element.70.refs_0_, f32[12576,768]{1,0:T(8,128)} %refs_1_.11, ...), custom_call_target="tpu_custom_call", output_to_operand_aliasing={{0}: (9, {}), {1}: (10, {}), {2}: (11, {}), {3}: (12, {})} | custom-call | flops 6082560000 | bytes 91238400 | tf_op jit(solution)/shard_map/pallas_call | solution.py:515
  315.2 2.0 collective-permute-start.9
  317.6 1.5 collective-permute-start.1
  319.2 2.6 collective-permute-done.9.refs_5_
  321.8 14.6 %shard_map.88 = (f32[12576,768]{1,0:T(8,128)}, f32[12576,768]{1,0:T(8,128)}, f32[12576,768]{1,0:T(8,128)}, bf16[12576,768]{1,0:T(8,128)(2,1)}, f32[8,128]{1,0:T(8,128)}) custom-call(f32[8,128]{1,0:T(8,128)} %get-tuple-element.76.refs_0_, f32[12576,768]{1,0:T(8,128)} %refs_1_.11, ...), custom_call_target="tpu_custom_call", output_to_operand_aliasing={{0}: (6, {}), {1}: (7, {}), {2}: (8, {}), {3}: (9, {})} | custom-call | flops 2433024000 | bytes 36495360 | tf_op jit(solution)/shard_map/pallas_call | solution.py:515
  336.4 35.8 %collective-permute-done.refs_4_ = f32[792,768]{1,0:T(8,128)S(1)} collective-permute-done((f32[792,768]{1,0:T(8,128)}, f32[792,768]{1,0:T(8,128)S(1)}, u32[]{:S(2)}, u32[]{:S(2)}) %collective-permute-start) | collective-permute-done | bytes 2433056 | tf_op jit(solution)/shard_map/ppermute | solution.py:569
  373.0 2.9 slice_select_fusion
  378.8 1.8 collective-permute-done.13.refs_7_
  380.6 1.5 copy-done.3
  382.1 26.2 %shard_map.89 = (f32[12576,768]{1,0:T(8,128)}, f32[12576,768]{1,0:T(8,128)}, f32[12576,768]{1,0:T(8,128)}, bf16[12576,768]{1,0:T(8,128)(2,1)}, f32[8,128]{1,0:T(8,128)}) custom-call(f32[8,128]{1,0:T(8,128)} %get-tuple-element.85.refs_0_, f32[12576,768]{1,0:T(8,128)} %refs_1_.11, ...), custom_call_target="tpu_custom_call", output_to_operand_aliasing={{0}: (8, {}), {1}: (9, {}), {2}: (10, {}), {3}: (11, {})} | custom-call | flops 4866048000 | bytes 72990720 | tf_op jit(solution)/shard_map/pallas_call | solution.py:515
  408.5 2.7 slice_select_fusion.1
  413.7 10.4 %shard_map.90 = (f32[12576,768]{1,0:T(8,128)}, f32[12576,768]{1,0:T(8,128)}, f32[12576,768]{1,0:T(8,128)}, bf16[12576,768]{1,0:T(8,128)(2,1)}, f32[8,128]{1,0:T(8,128)}) custom-call(f32[8,128]{1,0:T(8,128)} %get-tuple-element.91.refs_0_, f32[12576,768]{1,0:T(8,128)} %refs_1_.11, ...), custom_call_target="tpu_custom_call", output_to_operand_aliasing={{0}: (6, {}), {1}: (7, {}), {2}: (8, {}), {3}: (9, {})} | custom-call | flops 1622016000 | bytes 24330240 | tf_op jit(solution)/shard_map/pallas_call | solution.py:515
  424.2 2.3 collective-permute-done.15.refs_5_
  427.4 6.8 %shard_map.91 = (f32[12576,768]{1,0:T(8,128)}, f32[12576,768]{1,0:T(8,128)}, f32[12576,768]{1,0:T(8,128)}, bf16[12576,768]{1,0:T(8,128)(2,1)}, f32[8,128]{1,0:T(8,128)}) custom-call(f32[8,128]{1,0:T(8,128)} %get-tuple-element.98.refs_0_, f32[12576,768]{1,0:T(8,128)} %refs_1_.11, ...), custom_call_target="tpu_custom_call", output_to_operand_aliasing={{0}: (6, {}), {1}: (7, {}), {2}: (8, {}), {3}: (9, {})} | custom-call | flops 811008000 | bytes 12165120 | tf_op jit(solution)/shard_map/pallas_call | solution.py:515
  (47 shorter events, 13.3 us)
Async XLA Ops:
  0.6 6.8 %copy-start.8 = (s32[1,8,384]{2,1,0:T(8,128)S(1)}, s32[1,8,384]{2,1,0:T(8,128)}, u32[]{:S(2)}) copy-start(s32[1,8,384]{2,1,0:T(8,128)} %param.8) | copy-start | bytes 36868
  203.7 54.7 %collective-permute-start.2 = (f32[792,768]{1,0:T(8,128)}, f32[792,768]{1,0:T(8,128)S(1)}, u32[]{:S(2)}, u32[]{:S(2)}) collective-permute-start(f32[792,768]{1,0:T(8,128)} %get-tuple-element.68.refs_4_), channel_id=1, source_target_pairs={{0,2},{1,3},{2,0},{3,1},{4,6},{5,7},{6,4},{7,5},{8,10},{9,11},{10,... | collective-permute-start | bytes 7299080 | tf_op jit(solution)/shard_map/ppermute | solution.py:569
  203.8 55.1 %collective-permute-start.3 = (f32[792,768]{1,0:T(8,128)}, f32[792,768]{1,0:T(8,128)}, u32[]{:S(2)}, u32[]{:S(2)}) collective-permute-start(f32[792,768]{1,0:T(8,128)} %get-tuple-element.68.refs_4_), channel_id=1, source_target_pairs={{0,4},{4,0},{1,5},{5,1},{2,6},{6,2},{3,7},{7,3},{8,12},{12,8},{9,1... | collective-permute-start | bytes 7299080 | tf_op jit(solution)/shard_map/ppermute | solution.py:570
  205.5 57.0 %collective-permute-start.5 = (f32[792,768]{1,0:T(8,128)}, f32[792,768]{1,0:T(8,128)}, u32[]{:S(2)}, u32[]{:S(2)}) collective-permute-start(f32[792,768]{1,0:T(8,128)} %get-tuple-element.68.refs_4_), channel_id=1, source_target_pairs={{0,1},{1,0},{2,3},{3,2},{4,5},{5,4},{6,7},{7,6},{8,9},{9,8},{10,11... | collective-permute-start | bytes 7299080 | tf_op jit(solution)/shard_map/ppermute | solution.py:566
  258.3 24.7 %collective-permute-start.8 = (f32[792,768]{1,0:T(8,128)}, f32[792,768]{1,0:T(8,128)}, u32[]{:S(2)}, u32[]{:S(2)}) collective-permute-start(f32[792,768]{1,0:T(8,128)} %get-tuple-element.67.refs_5_), channel_id=1, source_target_pairs={{0,1},{1,0},{2,3},{3,2},{4,5},{5,4},{6,7},{7,6},{8,9},{9,8},{10,11... | collective-permute-start | bytes 7299080 | tf_op jit(solution)/shard_map/ppermute | solution.py:566
  258.5 24.5 %copy-start = (f32[792,768]{1,0:T(8,128)}, f32[792,768]{1,0:T(8,128)S(1)}, u32[]{:S(2)}) copy-start(f32[792,768]{1,0:T(8,128)S(1)} %collective-permute-done.2.refs_4_) | copy-start | bytes 7299076
  258.5 24.5 %collective-permute-start.6 = (f32[792,768]{1,0:T(8,128)S(1)}, f32[792,768]{1,0:T(8,128)}, u32[]{:S(2)}, u32[]{:S(2)}) collective-permute-start(f32[792,768]{1,0:T(8,128)S(1)} %collective-permute-done.2.refs_4_), channel_id=1, source_target_pairs={{0,1},{1,0},{2,3},{3,2},{4,5},{5,4},{6,7},{7,6},{8,9},{9,8},{10,11... | collective-permute-start | bytes 7299080 | tf_op jit(solution)/shard_map/ppermute | solution.py:566
  258.9 24.1 %collective-permute-start.7 = (f32[792,768]{1,0:T(8,128)}, f32[792,768]{1,0:T(8,128)}, u32[]{:S(2)}, u32[]{:S(2)}) collective-permute-start(f32[792,768]{1,0:T(8,128)} %collective-permute-done.3.refs_5_), channel_id=1, source_target_pairs={{0,1},{1,0},{2,3},{3,2},{4,5},{5,4},{6,7},{7,6},{8,9},{9,8},{10,11... | collective-permute-start | bytes 7299080 | tf_op jit(solution)/shard_map/ppermute | solution.py:566
  260.7 54.5 %collective-permute-start.4 = (f32[792,768]{1,0:T(8,128)}, f32[792,768]{1,0:T(8,128)}, u32[]{:S(2)}, u32[]{:S(2)}) collective-permute-start(f32[792,768]{1,0:T(8,128)} %broadcast_select_fusion), channel_id=1, source_target_pairs={{0,4},{1,3},{2,6},{3,1},{4,0},{5,7},{6,2},{7,5},{8,12},{9,11},{10,... | collective-permute-start | bytes 7299080 | tf_op jit(solution)/shard_map/ppermute | solution.py:574
  315.2 6.6 %collective-permute-start.9 = (f32[792,768]{1,0:T(8,128)}, f32[792,768]{1,0:T(8,128)}, u32[]{:S(2)}, u32[]{:S(2)}) collective-permute-start(f32[792,768]{1,0:T(8,128)} %collective-permute-done.4.refs_4_), channel_id=1, source_target_pairs={{0,1},{1,0},{2,3},{3,2},{4,5},{5,4},{6,7},{7,6},{8,9},{9,8},{10,11... | collective-permute-start | bytes 7299080 | tf_op jit(solution)/shard_map/ppermute | solution.py:566
  317.2 55.0 %collective-permute-start = (f32[792,768]{1,0:T(8,128)}, f32[792,768]{1,0:T(8,128)S(1)}, u32[]{:S(2)}, u32[]{:S(2)}) collective-permute-start(f32[792,768]{1,0:T(8,128)} %get-tuple-element.67.refs_5_), channel_id=1, source_target_pairs={{0,2},{1,3},{2,0},{3,1},{4,6},{5,7},{6,4},{7,5},{8,10},{9,11},{10,... | collective-permute-start | bytes 7299080 | tf_op jit(solution)/shard_map/ppermute | solution.py:569
  317.6 54.8 %collective-permute-start.1 = (f32[792,768]{1,0:T(8,128)}, f32[792,768]{1,0:T(8,128)}, u32[]{:S(2)}, u32[]{:S(2)}) collective-permute-start(f32[792,768]{1,0:T(8,128)} %get-tuple-element.67.refs_5_), channel_id=1, source_target_pairs={{0,4},{4,0},{1,5},{5,1},{2,6},{6,2},{3,7},{7,3},{8,12},{12,8},{9,1... | collective-permute-start | bytes 7299080 | tf_op jit(solution)/shard_map/ppermute | solution.py:570
  372.3 9.9 %copy-start.1 = (f32[792,768]{1,0:T(8,128)}, f32[792,768]{1,0:T(8,128)S(1)}, u32[]{:S(2)}) copy-start(f32[792,768]{1,0:T(8,128)S(1)} %collective-permute-done.refs_4_) | copy-start | bytes 7299076
  372.5 4.8 %collective-permute-start.12 = (f32[792,768]{1,0:T(8,128)S(1)}, f32[792,768]{1,0:T(8,128)S(1)}, u32[]{:S(2)}, u32[]{:S(2)}) collective-permute-start(f32[792,768]{1,0:T(8,128)S(1)} %collective-permute-done.refs_4_), channel_id=1, source_target_pairs={{0,1},{1,0},{2,3},{3,2},{4,5},{5,4},{6,7},{7,6},{8,9},{9,8},{10,11... | collective-permute-start | bytes 7299080 | tf_op jit(solution)/shard_map/ppermute | solution.py:566
  372.5 8.1 %collective-permute-start.13 = (f32[792,768]{1,0:T(8,128)}, f32[792,768]{1,0:T(8,128)S(1)}, u32[]{:S(2)}, u32[]{:S(2)}) collective-permute-start(f32[792,768]{1,0:T(8,128)} %collective-permute-done.1.refs_5_), channel_id=1, source_target_pairs={{0,1},{1,0},{2,3},{3,2},{4,5},{5,4},{6,7},{7,6},{8,9},{9,8},{10,11... | collective-permute-start | bytes 7299080 | tf_op jit(solution)/shard_map/ppermute | solution.py:566
  375.9 32.4 %collective-permute-start.11 = (f32[528,768]{1,0:T(8,128)}, f32[528,768]{1,0:T(8,128)S(1)}, u32[]{:S(2)}, u32[]{:S(2)}) collective-permute-start(f32[528,768]{1,0:T(8,128)} %slice_select_fusion), channel_id=1, source_target_pairs={{0,4},{1,3},{2,6},{3,1},{4,0},{5,7},{6,2},{7,5},{8,12},{9,11},{10,... | collective-permute-start | bytes 4866056 | tf_op jit(solution)/shard_map/ppermute | solution.py:574
  377.3 1.4 copy-start.2
  380.6 1.5 copy-start.3
  408.3 4.2 copy-start.4
  408.3 4.2 collective-permute-start.14
  411.2 12.9 %collective-permute-start.10 = (f32[264,768]{1,0:T(8,128)}, f32[264,768]{1,0:T(8,128)S(1)}, u32[]{:S(2)}, u32[]{:S(2)}) collective-permute-start(f32[264,768]{1,0:T(8,128)} %slice_select_fusion.1), channel_id=1, source_target_pairs={{0,4},{1,3},{2,6},{3,1},{4,0},{5,7},{6,2},{7,5},{8,12},{9,11},{10,... | collective-permute-start | bytes 2433032 | tf_op jit(solution)/shard_map/ppermute | solution.py:574
  412.5 1.2 copy-start.5
  424.1 2.4 copy-start.6
  424.1 2.4 collective-permute-start.15
  (1 other events, 0.9 us)

commit v2 on v1

--- a/solution.py
+++ b/solution.py
@@ -17,7 +17,7 @@
 OPT_STEP = 10
 
 ROW_STEP = 264
-TOK_STEP = 512
+TOK_STEP = 1024
 ADAMW_DEPTH = 4
 ADAMW_FLOPS = 2000
 VMEM_LIMIT = 60 * 1024 * 1024
@@ -99,12 +99,18 @@
     def _():
         def load_copy(i):
             place = pl.ds(pl.multiple_of(chunk(i) * size, size), size)
-            return pltpu.make_async_copy(act_ref.at[place], buf.at[core, span(0, i)], load.at[i])
+            return pltpu.make_async_copy(act_ref.at[place], hid_buf.at[pl.ds(i * size, size)], load.at[i])
+
+        def widen(i):
+            load_copy(i).wait()
+            buf[core, span(0, i), :] = hid_buf[i * size:(i + 1) * size, :].astype(jnp.float32)
 
         for i in range(n):
             load_copy(i).start()
+        widen(0)
         for i in range(n):
-            load_copy(i).wait()
+            if i + 1 < n:
+                widen(i + 1)
             if i < edge:
                 send(0, i, sx.at[i], recv.at[0, i], x_dev)
             if i < main:
@@ -548,7 +554,7 @@
         valid = jnp.minimum(own_rows, vocab - first_row)
         scal = jnp.stack([z * vocab + first_row, valid]).astype(jnp.int32)
 
-        acts = stage_acts.reshape(tok, dim).astype(jnp.float32)
+        acts = stage_acts.reshape(tok, dim)
         hid_bf, dx, all_ids, table_bf, top_own, sum_own = spread_call(acts, stage_ids.reshape(tok // 128, 128), master, own_rows, n_repl)
         ids, labels = all_ids[0].reshape(1, -1), all_ids[1].reshape(1, -1)
         rows_a = own_rows // (2 * ROW_STEP) * ROW_STEP

time: 435 us -> 428 us (0.984)
  other arithmetic: 15.5 us -> 8.61 us
    convert_element_type x1 -> x0, other arithmetic: 6.82 us -> none  [device_step(): acts = stage_acts.reshape(tok, dim).astype(jnp.float32)]
  transfers between devices with their start and end apart: 16 -> 16, of which waited for: 5 -> 5; matrix products, arithmetic and copies ran while one was open for 2% -> 2% of each run, Pallas kernels for 36% -> 37%
where the time goes in v2:
time: 428 us
  Pallas kernels  354 us (83%)
  waiting for transfers between devices  42.9 us (10%)
  starting transfers between devices  11.8 us (3%)
  local copies, waits for them, and re-layouts  9.27 us (2%)
  other arithmetic  8.61 us (2%)
    pallas_call x1, Pallas kernels, spread_call(): pl.pallas_call(functools.partial(spread_kernel, master.shape[0] - 7 * row...  140 us
    pallas_call x6, Pallas kernels, adamw_call(): pl.pallas_call(functools.partial(adamw_kernel, counts, spots, len(extra))...  110 us
    pallas_call x2, Pallas kernels, grad_call(): pl.pallas_call(functools.partial(grad_kernel, offset, tok_count), grid=(t...  62.8 us
    ppermute x2, waiting for transfers between devices, direct(): from_x = lax.ppermute(a, 'pp', x_swap)  35.8 us
    pallas_call x1, Pallas kernels, norm_call(): pl.pallas_call(functools.partial(norm_kernel, n_dev), in_specs=[vmem] * l...  21.2 us
    pallas_call x1, Pallas kernels, combine_call(): pl.pallas_call(functools.partial(combine_kernel, scale), in_specs=[pl.Blo...  19.2 us
  transfers between devices with their start and end apart: 16, of which 5 were waited for; matrix products, arithmetic and copies ran while one was open for 2% of the time, Pallas kernels for 37%

profile of v2, /device:TPU:0, one launch (start us, length us, event | category | flops | bytes accessed | tf_op | source)
XLA Modules:
  0.0 427.7 jit_solution(17915728373502124470)
XLA Ops:
  2.0 140.5 %spread.1 = (bf16[6144,768]{1,0:T(8,128)(2,1)}, f32[6144,768]{1,0:T(8,128)}, s32[2,2,24,128]{3,2,1,0:T(8,128)}, bf16[1584,768]{1,0:T(8,128)(2,1)}, f32[12,512]{1,0:T(8,128)}, /*index=5*/f32[12,512]{1,0:T(8,128)}) custom-call(bf16[3072,768]{1,0:T(8,128)(2,1)} %bitcast.7, s32[24,128]{1,0:T(8,128)} %reshape.27.ids_ref, f32[12576,768]{1,0:T(8,128)} %refs_1_.11), custom_call_target="tpu_custom_call" | custom-call | tf_op jit(solution)/shard_map/spread/pallas_call | solution.py:267
  144.6 19.2 %combine.1 = (f32[48,128]{1,0:T(8,128)}, f32[48,128]{1,0:T(8,128)}) custom-call(f32[96,128]{1,0:T(8,128)} %pad_maximum_fusion.in_ref), custom_call_target="tpu_custom_call" | custom-call | tf_op jit(solution)/shard_map/combine/pallas_call | solution.py:325
  165.9 31.3 %shard_map.85 = (f32[792,768]{1,0:T(8,128)}, f32[1,768]{1,0:T(1,128)}) custom-call(s32[2]{0:T(128)} %pad_add_fusion.scal_ref, bf16[1584,768]{1,0:T(8,128)(2,1)} %get-tuple-element.56.table_ref, bf16[6144,768]{1,0:T(8,128)(2,1)} %get-tuple-element.57.hid_ref, f32[6144,768]{1,0:T(8,128)} %get-tuple-element.58.dx_ref, f32[1,6144]{1,0:T(1,128)} %bitcast.12, ...), custom_call_target="tpu_custom_call" | custom-call | flops 22422749184 | bytes 28311552 | tf_op jit(solution)/shard_map/pallas_call | solution.py:413
  197.2 1.8 collective-permute-start.3
  198.9 31.6 %shard_map.84 = (f32[792,768]{1,0:T(8,128)}, f32[1,768]{1,0:T(1,128)}) custom-call(s32[2]{0:T(128)} %pad_add_fusion.scal_ref, bf16[1584,768]{1,0:T(8,128)(2,1)} %get-tuple-element.56.table_ref, bf16[6144,768]{1,0:T(8,128)(2,1)} %get-tuple-element.57.hid_ref, f32[6144,768]{1,0:T(8,128)} %get-tuple-element.58.dx_ref, f32[1,6144]{1,0:T(1,128)} %bitcast.13, ...), custom_call_target="tpu_custom_call" | custom-call | flops 22422749184 | bytes 28311552 | tf_op jit(solution)/shard_map/pallas_call | solution.py:413
  230.5 21.2 %norm.1.refs_0_ = f32[8,128]{1,0:T(8,128)} custom-call(f32[1,768]{1,0:T(1,128)} %get-tuple-element.65.refs_0_, f32[1,768]{1,0:T(1,128)} %get-tuple-element.66.refs_1_), custom_call_target="tpu_custom_call" | custom-call | tf_op jit(solution)/shard_map/norm/pallas_call | solution.py:363
  252.4 1.8 broadcast_select_fusion
  254.1 1.8 collective-permute-start.4
  255.9 20.4 %shard_map.86 = (f32[12576,768]{1,0:T(8,128)}, f32[12576,768]{1,0:T(8,128)}, f32[12576,768]{1,0:T(8,128)}, bf16[12576,768]{1,0:T(8,128)(2,1)}, f32[8,128]{1,0:T(8,128)}) custom-call(f32[8,128]{1,0:T(8,128)} %norm.1.refs_0_, f32[12576,768]{1,0:T(8,128)} %refs_1_.11, f32[12576,768]{1,0:T(8,128)} %refs_2_.11, f32[12576,768]{1,0:T(8,128)} %refs_3_.11, ...), custom_call_target="tpu_custom_call" | custom-call | flops 3649536000 | bytes 54743040 | tf_op jit(solution)/shard_map/pallas_call | solution.py:521
  276.4 32.2 %shard_map.87 = (f32[12576,768]{1,0:T(8,128)}, f32[12576,768]{1,0:T(8,128)}, f32[12576,768]{1,0:T(8,128)}, bf16[12576,768]{1,0:T(8,128)(2,1)}, f32[8,128]{1,0:T(8,128)}) custom-call(f32[8,128]{1,0:T(8,128)} %get-tuple-element.70.refs_0_, f32[12576,768]{1,0:T(8,128)} %refs_1_.11, ...), custom_call_target="tpu_custom_call", output_to_operand_aliasing={{0}: (9, {}), {1}: (10, {}), {2}: (11, {}), {3}: (12, {})} | custom-call | flops 6082560000 | bytes 91238400 | tf_op jit(solution)/shard_map/pallas_call | solution.py:521
  308.6 2.0 collective-permute-start.9
  311.0 1.5 collective-permute-start.1
  312.6 2.6 collective-permute-done.9.refs_5_
  315.2 14.6 %shard_map.88 = (f32[12576,768]{1,0:T(8,128)}, f32[12576,768]{1,0:T(8,128)}, f32[12576,768]{1,0:T(8,128)}, bf16[12576,768]{1,0:T(8,128)(2,1)}, f32[8,128]{1,0:T(8,128)}) custom-call(f32[8,128]{1,0:T(8,128)} %get-tuple-element.76.refs_0_, f32[12576,768]{1,0:T(8,128)} %refs_1_.11, ...), custom_call_target="tpu_custom_call", output_to_operand_aliasing={{0}: (6, {}), {1}: (7, {}), {2}: (8, {}), {3}: (9, {})} | custom-call | flops 2433024000 | bytes 36495360 | tf_op jit(solution)/shard_map/pallas_call | solution.py:521
  329.8 35.8 %collective-permute-done.refs_4_ = f32[792,768]{1,0:T(8,128)S(1)} collective-permute-done((f32[792,768]{1,0:T(8,128)}, f32[792,768]{1,0:T(8,128)S(1)}, u32[]{:S(2)}, u32[]{:S(2)}) %collective-permute-start) | collective-permute-done | bytes 2433056 | tf_op jit(solution)/shard_map/ppermute | solution.py:575
  366.4 2.9 slice_select_fusion
  369.3 1.5 collective-permute-start.11
  372.2 1.8 collective-permute-done.13.refs_7_
  374.0 1.5 copy-done.3
  375.5 26.2 %shard_map.89 = (f32[12576,768]{1,0:T(8,128)}, f32[12576,768]{1,0:T(8,128)}, f32[12576,768]{1,0:T(8,128)}, bf16[12576,768]{1,0:T(8,128)(2,1)}, f32[8,128]{1,0:T(8,128)}) custom-call(f32[8,128]{1,0:T(8,128)} %get-tuple-element.85.refs_0_, f32[12576,768]{1,0:T(8,128)} %refs_1_.11, ...), custom_call_target="tpu_custom_call", output_to_operand_aliasing={{0}: (8, {}), {1}: (9, {}), {2}: (10, {}), {3}: (11, {})} | custom-call | flops 4866048000 | bytes 72990720 | tf_op jit(solution)/shard_map/pallas_call | solution.py:521
  401.9 2.7 slice_select_fusion.1
  407.1 10.3 %shard_map.90 = (f32[12576,768]{1,0:T(8,128)}, f32[12576,768]{1,0:T(8,128)}, f32[12576,768]{1,0:T(8,128)}, bf16[12576,768]{1,0:T(8,128)(2,1)}, f32[8,128]{1,0:T(8,128)}) custom-call(f32[8,128]{1,0:T(8,128)} %get-tuple-element.91.refs_0_, f32[12576,768]{1,0:T(8,128)} %refs_1_.11, ...), custom_call_target="tpu_custom_call", output_to_operand_aliasing={{0}: (6, {}), {1}: (7, {}), {2}: (8, {}), {3}: (9, {})} | custom-call | flops 1622016000 | bytes 24330240 | tf_op jit(solution)/shard_map/pallas_call | solution.py:521
  417.6 2.3 collective-permute-done.15.refs_5_
  420.8 6.7 %shard_map.91 = (f32[12576,768]{1,0:T(8,128)}, f32[12576,768]{1,0:T(8,128)}, f32[12576,768]{1,0:T(8,128)}, bf16[12576,768]{1,0:T(8,128)(2,1)}, f32[8,128]{1,0:T(8,128)}) custom-call(f32[8,128]{1,0:T(8,128)} %get-tuple-element.98.refs_0_, f32[12576,768]{1,0:T(8,128)} %refs_1_.11, ...), custom_call_target="tpu_custom_call", output_to_operand_aliasing={{0}: (6, {}), {1}: (7, {}), {2}: (8, {}), {3}: (9, {})} | custom-call | flops 811008000 | bytes 12165120 | tf_op jit(solution)/shard_map/pallas_call | solution.py:521
  (44 shorter events, 12.5 us)
Async XLA Ops:
  197.1 54.7 %collective-permute-start.2 = (f32[792,768]{1,0:T(8,128)}, f32[792,768]{1,0:T(8,128)S(1)}, u32[]{:S(2)}, u32[]{:S(2)}) collective-permute-start(f32[792,768]{1,0:T(8,128)} %get-tuple-element.68.refs_4_), channel_id=1, source_target_pairs={{0,2},{1,3},{2,0},{3,1},{4,6},{5,7},{6,4},{7,5},{8,10},{9,11},{10,... | collective-permute-start | bytes 7299080 | tf_op jit(solution)/shard_map/ppermute | solution.py:575
  197.2 55.1 %collective-permute-start.3 = (f32[792,768]{1,0:T(8,128)}, f32[792,768]{1,0:T(8,128)}, u32[]{:S(2)}, u32[]{:S(2)}) collective-permute-start(f32[792,768]{1,0:T(8,128)} %get-tuple-element.68.refs_4_), channel_id=1, source_target_pairs={{0,4},{4,0},{1,5},{5,1},{2,6},{6,2},{3,7},{7,3},{8,12},{12,8},{9,1... | collective-permute-start | bytes 7299080 | tf_op jit(solution)/shard_map/ppermute | solution.py:576
  198.9 57.0 %collective-permute-start.5 = (f32[792,768]{1,0:T(8,128)}, f32[792,768]{1,0:T(8,128)}, u32[]{:S(2)}, u32[]{:S(2)}) collective-permute-start(f32[792,768]{1,0:T(8,128)} %get-tuple-element.68.refs_4_), channel_id=1, source_target_pairs={{0,1},{1,0},{2,3},{3,2},{4,5},{5,4},{6,7},{7,6},{8,9},{9,8},{10,11... | collective-permute-start | bytes 7299080 | tf_op jit(solution)/shard_map/ppermute | solution.py:572
  251.7 24.6 %collective-permute-start.8 = (f32[792,768]{1,0:T(8,128)}, f32[792,768]{1,0:T(8,128)}, u32[]{:S(2)}, u32[]{:S(2)}) collective-permute-start(f32[792,768]{1,0:T(8,128)} %get-tuple-element.67.refs_5_), channel_id=1, source_target_pairs={{0,1},{1,0},{2,3},{3,2},{4,5},{5,4},{6,7},{7,6},{8,9},{9,8},{10,11... | collective-permute-start | bytes 7299080 | tf_op jit(solution)/shard_map/ppermute | solution.py:572
  251.9 24.5 %copy-start = (f32[792,768]{1,0:T(8,128)}, f32[792,768]{1,0:T(8,128)S(1)}, u32[]{:S(2)}) copy-start(f32[792,768]{1,0:T(8,128)S(1)} %collective-permute-done.2.refs_4_) | copy-start | bytes 7299076
  251.9 24.5 %collective-permute-start.6 = (f32[792,768]{1,0:T(8,128)S(1)}, f32[792,768]{1,0:T(8,128)}, u32[]{:S(2)}, u32[]{:S(2)}) collective-permute-start(f32[792,768]{1,0:T(8,128)S(1)} %collective-permute-done.2.refs_4_), channel_id=1, source_target_pairs={{0,1},{1,0},{2,3},{3,2},{4,5},{5,4},{6,7},{7,6},{8,9},{9,8},{10,11... | collective-permute-start | bytes 7299080 | tf_op jit(solution)/shard_map/ppermute | solution.py:572
  252.3 24.1 %collective-permute-start.7 = (f32[792,768]{1,0:T(8,128)}, f32[792,768]{1,0:T(8,128)}, u32[]{:S(2)}, u32[]{:S(2)}) collective-permute-start(f32[792,768]{1,0:T(8,128)} %collective-permute-done.3.refs_5_), channel_id=1, source_target_pairs={{0,1},{1,0},{2,3},{3,2},{4,5},{5,4},{6,7},{7,6},{8,9},{9,8},{10,11... | collective-permute-start | bytes 7299080 | tf_op jit(solution)/shard_map/ppermute | solution.py:572
  254.1 54.5 %collective-permute-start.4 = (f32[792,768]{1,0:T(8,128)}, f32[792,768]{1,0:T(8,128)}, u32[]{:S(2)}, u32[]{:S(2)}) collective-permute-start(f32[792,768]{1,0:T(8,128)} %broadcast_select_fusion), channel_id=1, source_target_pairs={{0,4},{1,3},{2,6},{3,1},{4,0},{5,7},{6,2},{7,5},{8,12},{9,11},{10,... | collective-permute-start | bytes 7299080 | tf_op jit(solution)/shard_map/ppermute | solution.py:580
  308.6 6.6 %collective-permute-start.9 = (f32[792,768]{1,0:T(8,128)}, f32[792,768]{1,0:T(8,128)}, u32[]{:S(2)}, u32[]{:S(2)}) collective-permute-start(f32[792,768]{1,0:T(8,128)} %collective-permute-done.4.refs_4_), channel_id=1, source_target_pairs={{0,1},{1,0},{2,3},{3,2},{4,5},{5,4},{6,7},{7,6},{8,9},{9,8},{10,11... | collective-permute-start | bytes 7299080 | tf_op jit(solution)/shard_map/ppermute | solution.py:572
  310.6 55.0 %collective-permute-start = (f32[792,768]{1,0:T(8,128)}, f32[792,768]{1,0:T(8,128)S(1)}, u32[]{:S(2)}, u32[]{:S(2)}) collective-permute-start(f32[792,768]{1,0:T(8,128)} %get-tuple-element.67.refs_5_), channel_id=1, source_target_pairs={{0,2},{1,3},{2,0},{3,1},{4,6},{5,7},{6,4},{7,5},{8,10},{9,11},{10,... | collective-permute-start | bytes 7299080 | tf_op jit(solution)/shard_map/ppermute | solution.py:575
  311.0 54.8 %collective-permute-start.1 = (f32[792,768]{1,0:T(8,128)}, f32[792,768]{1,0:T(8,128)}, u32[]{:S(2)}, u32[]{:S(2)}) collective-permute-start(f32[792,768]{1,0:T(8,128)} %get-tuple-element.67.refs_5_), channel_id=1, source_target_pairs={{0,4},{4,0},{1,5},{5,1},{2,6},{6,2},{3,7},{7,3},{8,12},{12,8},{9,1... | collective-permute-start | bytes 7299080 | tf_op jit(solution)/shard_map/ppermute | solution.py:576
  365.6 9.9 %copy-start.1 = (f32[792,768]{1,0:T(8,128)}, f32[792,768]{1,0:T(8,128)S(1)}, u32[]{:S(2)}) copy-start(f32[792,768]{1,0:T(8,128)S(1)} %collective-permute-done.refs_4_) | copy-start | bytes 7299076
  365.9 4.8 %collective-permute-start.12 = (f32[792,768]{1,0:T(8,128)S(1)}, f32[792,768]{1,0:T(8,128)S(1)}, u32[]{:S(2)}, u32[]{:S(2)}) collective-permute-start(f32[792,768]{1,0:T(8,128)S(1)} %collective-permute-done.refs_4_), channel_id=1, source_target_pairs={{0,1},{1,0},{2,3},{3,2},{4,5},{5,4},{6,7},{7,6},{8,9},{9,8},{10,11... | collective-permute-start | bytes 7299080 | tf_op jit(solution)/shard_map/ppermute | solution.py:572
  365.9 8.1 %collective-permute-start.13 = (f32[792,768]{1,0:T(8,128)}, f32[792,768]{1,0:T(8,128)S(1)}, u32[]{:S(2)}, u32[]{:S(2)}) collective-permute-start(f32[792,768]{1,0:T(8,128)} %collective-permute-done.1.refs_5_), channel_id=1, source_target_pairs={{0,1},{1,0},{2,3},{3,2},{4,5},{5,4},{6,7},{7,6},{8,9},{9,8},{10,11... | collective-permute-start | bytes 7299080 | tf_op jit(solution)/shard_map/ppermute | solution.py:572
  369.3 32.4 %collective-permute-start.11 = (f32[528,768]{1,0:T(8,128)}, f32[528,768]{1,0:T(8,128)S(1)}, u32[]{:S(2)}, u32[]{:S(2)}) collective-permute-start(f32[528,768]{1,0:T(8,128)} %slice_select_fusion), channel_id=1, source_target_pairs={{0,4},{1,3},{2,6},{3,1},{4,0},{5,7},{6,2},{7,5},{8,12},{9,11},{10,... | collective-permute-start | bytes 4866056 | tf_op jit(solution)/shard_map/ppermute | solution.py:580
  370.7 1.5 copy-start.2
  374.0 1.5 copy-start.3
  401.7 4.2 copy-start.4
  401.7 4.2 collective-permute-start.14
  404.6 12.8 %collective-permute-start.10 = (f32[264,768]{1,0:T(8,128)}, f32[264,768]{1,0:T(8,128)S(1)}, u32[]{:S(2)}, u32[]{:S(2)}) collective-permute-start(f32[264,768]{1,0:T(8,128)} %slice_select_fusion.1), channel_id=1, source_target_pairs={{0,4},{1,3},{2,6},{3,1},{4,0},{5,7},{6,2},{7,5},{8,12},{9,11},{10,... | collective-permute-start | bytes 2433032 | tf_op jit(solution)/shard_map/ppermute | solution.py:580
  405.9 1.2 copy-start.5
  417.5 2.4 copy-start.6
  417.5 2.4 collective-permute-start.15
  419.9 0.9 copy-start.7
